TPU v7x, 64 devices: a 2x2x8 block of a 4x4x8 slice. The times are simulated.
64 devices in a mesh: rep: 4 (over x, y), dp: 16 (over z, core).
Axes of the slice: x: 2, y: 2, z: 8, core: 2. Of those that a mesh axis runs over, the one named last changes fastest.
The devices are a block of a 4x4x8 slice.
Arguments:
- hidden: bfloat16 [2048, 2048], P(('rep', 'dp')), parts along dimension 0
- ckv_cache: bfloat16 [2048, 128, 512], P(('rep', 'dp')), parts along dimension 0
- kr_cache: bfloat16 [2048, 128, 64], P(('rep', 'dp')), parts along dimension 0
- seq_lens: int32 [2048], P(('rep', 'dp')), parts along dimension 0
- expert_ids: int32 [2048, 6], P(('rep', 'dp')), parts along dimension 0
- attn_gain: bfloat16 [2048], replicated
- kv_gain: bfloat16 [512], replicated
- moe_gain: bfloat16 [2048], replicated
- w_q: bfloat16 [2048, 3072], replicated
- w_dkv: bfloat16 [2048, 576], replicated
- w_uk: bfloat16 [16, 128, 512], replicated
- w_uv: bfloat16 [16, 512, 128], replicated
- w_o: bfloat16 [2048, 2048], replicated
- w_router: bfloat16 [2048, 64], replicated
- shared_gate: bfloat16 [2048, 2816], replicated
- shared_up: bfloat16 [2048, 2816], replicated
- shared_down: bfloat16 [2816, 2048], replicated
- expert_gate: bfloat16 [64, 2048, 1408], P('dp')
- expert_up: bfloat16 [64, 2048, 1408], P('dp')
- expert_down: bfloat16 [64, 1408, 2048], P('dp')
Outputs:
- output 1: bfloat16 [2048, 2048], P(('rep', 'dp')), parts along dimension 0
- output 2: bfloat16 [2048, 512], P(('rep', 'dp')), parts along dimension 0
- output 3: bfloat16 [2048, 64], P(('rep', 'dp')), parts along dimension 0
There are 4 independent parts. A program takes and returns all parts, laid end to end along the dimension named above; an argument that names none is the same for every part.
All inputs are finite; a program needn't handle non-finite values.
Results may differ from a plain program's by a relative error of at most 0.0123531.
Values are sent between devices in bfloat16 or wider.
A program may use at most 768 MiB of HBM per device.

v0:
```python
import jax
import jax.numpy as jnp
from jax import lax
from jax.sharding import PartitionSpec as P

NORM_EPS = 1e-6
ROPE_THETA = 10000.0


def rms_norm(values, gain_vec):
    vals_f32 = values.astype(jnp.float32)
    inv_rms = lax.rsqrt(jnp.mean(vals_f32 * vals_f32, axis=-1, keepdims=True) + NORM_EPS)
    return (vals_f32 * inv_rms * gain_vec.astype(jnp.float32)).astype(jnp.bfloat16)


def rope_tables(positions, rope_dim):
    inv_freq = ROPE_THETA ** (-2.0 * jnp.arange(rope_dim // 2, dtype=jnp.float32) / rope_dim)
    angles = positions.astype(jnp.float32)[:, None] * inv_freq[None, :]
    return jnp.cos(angles), jnp.sin(angles)


def apply_rope(values, rope_cos, rope_sin):
    half_dim = values.shape[-1] // 2
    first_half = values[..., :half_dim]
    second_half = values[..., half_dim:]
    return jnp.concatenate([first_half * rope_cos - second_half * rope_sin, second_half * rope_cos + first_half * rope_sin], axis=-1)


def attention_block(hidden, ckv_cache, kr_cache, seq_lens, attn_gain, kv_gain, w_q, w_dkv, w_uk, w_uv, w_o):
    batch_rows = hidden.shape[0]
    num_heads, nope_dim, value_a8 = w_uk.shape
    rope_dim = kr_cache.shape[-1]
    cache_len = ckv_cache.shape[1]
    score_scale = (nope_dim + rope_dim) ** -0.5
    normed_x = rms_norm(hidden, attn_gain)
    q_all = jnp.dot(normed_x, w_q, preferred_element_type=jnp.float32).astype(jnp.bfloat16).reshape(batch_rows, num_heads, nope_dim + rope_dim)
    latent_kv = jnp.dot(normed_x, w_dkv, preferred_element_type=jnp.float32)
    ckv_new = rms_norm(latent_kv[:, :value_a8], kv_gain)
    rope_cos, rope_sin = rope_tables(seq_lens, rope_dim)
    kr_new = apply_rope(latent_kv[:, value_a8:], rope_cos, rope_sin).astype(jnp.bfloat16)
    q_rot = apply_rope(q_all[:, :, nope_dim:].astype(jnp.float32), rope_cos[:, None, :], rope_sin[:, None, :]).astype(jnp.bfloat16)
    q_lat = jnp.einsum('bhn,hnc->bhc', q_all[:, :, :nope_dim], w_uk, preferred_element_type=jnp.float32).astype(jnp.bfloat16)
    scores = (jnp.einsum('bhc,blc->bhl', q_lat, ckv_cache, preferred_element_type=jnp.float32) + jnp.einsum('bhr,blr->bhl', q_rot, kr_cache, preferred_element_type=jnp.float32)) * score_scale
    valid_mask = jnp.arange(cache_len)[None, None, :] < seq_lens[:, None, None]
    scores = jnp.where(valid_mask, scores, -jnp.inf)
    new_score = (jnp.einsum('bhc,bc->bh', q_lat, ckv_new, preferred_element_type=jnp.float32) + jnp.einsum('bhr,br->bh', q_rot, kr_new, preferred_element_type=jnp.float32)) * score_scale
    top_score = jnp.maximum(jnp.max(scores, axis=-1), new_score)
    exp_cache = jnp.exp(scores - top_score[:, :, None])
    exp_new = jnp.exp(new_score - top_score)
    denominator = jnp.sum(exp_cache, axis=-1) + exp_new
    prob_cache = (exp_cache / denominator[:, :, None]).astype(jnp.bfloat16)
    prob_new = (exp_new / denominator).astype(jnp.bfloat16)
    o_lat = (jnp.einsum('bhl,blc->bhc', prob_cache, ckv_cache, preferred_element_type=jnp.float32) + jnp.einsum('bh,bc->bhc', prob_new, ckv_new, preferred_element_type=jnp.float32)).astype(jnp.bfloat16)
    head_out = jnp.einsum('bhc,hcv->bhv', o_lat, w_uv, preferred_element_type=jnp.float32).astype(jnp.bfloat16).reshape(batch_rows, -1)
    resid_out = (hidden.astype(jnp.float32) + jnp.dot(head_out, w_o, preferred_element_type=jnp.float32)).astype(jnp.bfloat16)
    return resid_out, ckv_new, kr_new


def route_tables(expert_ids, num_experts, capacity):
    batch_rows, top_k = expert_ids.shape
    picked = expert_ids[:, :, None] == jnp.arange(num_experts)[None, None, :]
    pick_flat = picked.reshape(batch_rows * top_k, num_experts)
    pick_int = pick_flat.astype(jnp.int32)
    slot_rank = jnp.sum((jnp.cumsum(pick_int, axis=0) - pick_int) * pick_int, axis=-1)
    slot_hit = slot_rank[:, None] == jnp.arange(capacity)[None, :]
    slot_place = (pick_flat[:, :, None] & slot_hit[:, None, :]).reshape(batch_rows, top_k, num_experts * capacity)
    return picked, slot_place


def moe_block(resid_out, expert_ids, capacity, moe_gain, w_router, shared_gate, shared_up, shared_down, expert_gate, expert_up, expert_down):
    batch_rows, model_width = resid_out.shape
    top_k = expert_ids.shape[1]
    num_experts = w_router.shape[1]
    local_experts = expert_gate.shape[0]
    group_size = num_experts // local_experts
    moe_in = rms_norm(resid_out, moe_gain)
    router_prob = jax.nn.softmax(jnp.dot(moe_in, w_router, preferred_element_type=jnp.float32), axis=-1)
    picked, slot_place = route_tables(expert_ids, num_experts, capacity)
    gate_vals = jnp.sum(jnp.where(picked, router_prob[:, None, :], 0.0), axis=-1)
    shared_act = (jax.nn.silu(jnp.dot(moe_in, shared_gate, preferred_element_type=jnp.float32)) * jnp.dot(moe_in, shared_up, preferred_element_type=jnp.float32)).astype(jnp.bfloat16)
    shared_out = jnp.dot(shared_act, shared_down, preferred_element_type=jnp.float32)
    dispatch = jnp.any(slot_place, axis=1).astype(jnp.bfloat16)
    send_rows = jnp.einsum('tx,tm->xm', dispatch, moe_in, preferred_element_type=jnp.float32).astype(jnp.bfloat16).reshape(group_size, local_experts, capacity, model_width)
    recv_rows = lax.all_to_all(send_rows, 'dp', 0, 0, tiled=True)
    gate_act = jnp.einsum('secm,emf->secf', recv_rows, expert_gate, preferred_element_type=jnp.float32)
    up_act = jnp.einsum('secm,emf->secf', recv_rows, expert_up, preferred_element_type=jnp.float32)
    mid_act = (jax.nn.silu(gate_act) * up_act).astype(jnp.bfloat16)
    expert_rows = jnp.einsum('secf,efm->secm', mid_act, expert_down, preferred_element_type=jnp.float32).astype(jnp.bfloat16)
    back_rows = lax.all_to_all(expert_rows, 'dp', 0, 0, tiled=True).reshape(num_experts * capacity, model_width)
    choice_rows = jnp.dot(slot_place.reshape(batch_rows * top_k, num_experts * capacity).astype(jnp.bfloat16), back_rows, preferred_element_type=jnp.float32).reshape(batch_rows, top_k, model_width)
    routed_out = jnp.sum(gate_vals[:, :, None] * choice_rows, axis=1)
    return (resid_out.astype(jnp.float32) + shared_out + routed_out).astype(jnp.bfloat16)


def solution(mesh):
    row_spec = P(('rep', 'dp'))
    full_spec = P()
    expert_spec = P('dp')

    def device_step(hidden, ckv_cache, kr_cache, seq_lens, expert_ids, attn_gain, kv_gain, moe_gain, w_q, w_dkv, w_uk, w_uv, w_o, w_router, shared_gate, shared_up, shared_down, expert_gate, expert_up, expert_down):
        capacity = max(2, 2 * hidden.shape[0] * expert_ids.shape[1] // w_router.shape[1])
        resid_out, ckv_new, kr_new = attention_block(hidden, ckv_cache, kr_cache, seq_lens, attn_gain, kv_gain, w_q, w_dkv, w_uk, w_uv, w_o)
        layer_out = moe_block(resid_out, expert_ids, capacity, moe_gain, w_router, shared_gate, shared_up, shared_down, expert_gate, expert_up, expert_down)
        return layer_out, ckv_new, kr_new

    in_specs = (row_spec,) * 5 + (full_spec,) * 12 + (expert_spec,) * 3
    return jax.shard_map(device_step, mesh=mesh, in_specs=in_specs, out_specs=(row_spec, row_spec, row_spec), check_vma=False)
```

profile of v0, /device:TPU:22, one launch (start us, length us, event | category | flops | bytes accessed | tf_op | source)
XLA Modules:
  0.0 184.5 jit_solution(10466743856630989475)
XLA Ops:
  0.6 0.9 copy.72
  1.7 0.7 convert_element_type.86
  2.4 1.0 fusion.48
  3.5 7.0 %convolution_convert_fusion = bf16[32,3072]{1,0:T(8,128)(2,1)S(1)} fusion(bf16[2048,3072]{1,0:T(8,128)(2,1)} %param.28, bf16[32,2048]{1,0:T(8,128)(2,1)} %param.20, f32[2048]{0:T(1024)S(1)} %convert_element_type.86, f32[32]{0:T(128)S(1)} %add_rsqrt_fusion.2), kind=kOutput, calls=%fused_computation.8 | convolution fusion | flops 403013632 | bytes 12918912 | tf_op jit(solution)/shard_map/dot_general | solution.py:36
  11.0 0.8 reduce-window.6
  12.4 4.1 %broadcast_and_fusion = pred[192,64,6]{2,1,0:T(8,128)(4,1)} fusion(pred[192,6]{1,0:T(8,128)(4,1)S(1)} %iota_compare_fusion, pred[192,64]{1,0:T(8,128)(4,1)S(1)} %copy.73), kind=kLoop, calls=%fused_computation.9 | loop fusion | flops 73728 | bytes 87168 | tf_op jit(solution)/shard_map/and | solution.py:66
  16.5 5.3 %and.29 = pred[32,6,384]{2,1,0:T(8,128)(4,1)S(1)} reshape(pred[192,64,6]{2,1,0:T(8,128)(4,1)} %broadcast_and_fusion) | data formatting | bytes 147456 | tf_op jit(solution)/shard_map/and | solution.py:66
  21.8 0.8 fusion.61
  22.8 2.2 %fusion.33 = bf16[32,16,512]{2,0,1:T(8,128)(2,1)S(1)} fusion(bf16[16,128,512]{2,1,0:T(8,128)(2,1)} %param.30, bf16[32,16,128]{2,1,0:T(8,128)(2,1)S(1)} %slice.43), kind=kOutput, calls=%fused_computation.30 | convolution fusion | flops 67371008 | bytes 2752512 | tf_op jit(solution)/shard_map/bhn,hnc->bhc/dot_general | solution.py:42
  25.1 1.2 fusion.40
  26.3 0.4 fusion.38
  27.4 0.4 fusion.77
  28.1 0.7 fusion.32
  28.8 1.2 copy-done.4
  30.1 0.7 fusion.36
  30.8 1.7 multiply_reduce_fusion
  32.6 1.8 convolution_convert_fusion.1
  34.4 2.5 %reshape.192 = bf16[16,4,6,2048]{3,2,1,0:T(8,128)(2,1)S(1)} reshape(bf16[384,2048]{1,0:T(8,128)(2,1)} %convolution_convert_fusion.1) | data formatting | bytes 3145728 | tf_op jit(solution)/shard_map/reshape | solution.py:83
  36.9 1.3 copy.76
  38.2 48.7 %all_to_all.10 = bf16[16,4,6,2048]{3,1,2,0:T(4,128)(2,1)S(1)} all-to-all(bf16[16,4,6,2048]{3,1,2,0:T(4,128)(2,1)S(1)} %copy.76), channel_id=1, replica_groups=mesh['rep'=4,'dp'=16] {'dp'}, dimensions={0} | all-to-all | bytes 3145728 | tf_op jit(solution)/shard_map/all_to_all | solution.py:84
  86.9 10.1 %fusion.7 = f32[16,4,6,1408]{3,0,2,1:T(8,128)S(1)} fusion(bf16[4,2048,1408]{2,1,0:T(8,128)(2,1)} %param.37, bf16[16,4,6,2048]{3,1,2,0:T(4,128)(2,1)S(1)} %all_to_all.10), kind=kOutput, calls=%fused_computation.10 | convolution fusion | flops 2214592512 | bytes 26804224 | tf_op jit(solution)/shard_map/secm,emf->secf/dot_general | solution.py:85
  97.0 12.7 %fusion.19 = bf16[16,4,6,1408]{3,0,2,1:T(8,128)(2,1)S(1)} fusion(bf16[4,2048,1408]{2,1,0:T(8,128)(2,1)} %param.38, f32[16,4,6,1408]{3,0,2,1:T(8,128)S(1)} %fusion.7, bf16[16,4,6,2048]{3,1,2,0:T(4,128)(2,1)S(1)} %all_to_all.10), kind=kOutput, calls=%fused_computation.15 | convolution fusion | flops 2217836544 | bytes 27885568 | tf_op jit(solution)/shard_map/secm,emf->secf/dot_general | solution.py:86
  109.7 11.5 %fusion.22 = bf16[16,4,6,2048]{3,0,2,1:T(8,128)(2,1)S(1)} fusion(bf16[16,4,6,1408]{3,0,2,1:T(8,128)(2,1)S(1)} %fusion.19, bf16[4,1408,2048]{2,1,0:T(8,128)(2,1)} %param.39), kind=kOutput, calls=%fused_computation.16 | convolution fusion | flops 2215378944 | bytes 25722880 | tf_op jit(solution)/shard_map/secf,efm->secm/dot_general | solution.py:88
  121.3 2.4 %copy.79 = bf16[16,4,6,2048]{3,1,2,0:T(4,128)(2,1)} copy(bf16[16,4,6,2048]{3,0,2,1:T(8,128)(2,1)S(1)} %fusion.22) | data formatting | bytes 3145728 | tf_op jit(solution)/shard_map/convert_element_type | solution.py:88
  123.6 5.2 %all-to-all-start.1 = ((bf16[16,4,6,2048]{3,1,2,0:T(4,128)(2,1)}), bf16[16,4,6,2048]{3,1,2,0:T(4,128)(2,1)}, u32[]{:S(2)}, u32[]{:S(2)}) async-start(bf16[16,4,6,2048]{3,1,2,0:T(4,128)(2,1)} %copy.79), calls=%async_computation.1 | async-start | bytes 3145728 | tf_op jit(solution)/shard_map/all_to_all | solution.py:89
  128.8 0.7 pad_maximum_fusion.3
  130.3 6.4 %fusion.75 = f32[32,2816]{1,0:T(8,128)S(1)} fusion(bf16[2048,2816]{1,0:T(8,128)(2,1)} %param.34, f32[32,2048]{1,0:T(8,128)S(1)} %get-tuple-element.16, f32[2048]{0:T(1024)S(1)} %convert_element_type.102, f32[32]{0:T(128)S(1)} %add_rsqrt_fusion), kind=kOutput, calls=%fused_computation.109 | convolution fusion | flops 369295360 | bytes 12165248 | tf_op jit(solution)/shard_map/dot_general | solution.py:80
  136.8 29.2 %all-to-all-done.1 = bf16[16,4,6,2048]{3,1,2,0:T(4,128)(2,1)} async-done(((bf16[16,4,6,2048]{3,1,2,0:T(4,128)(2,1)}), bf16[16,4,6,2048]{3,1,2,0:T(4,128)(2,1)}, u32[]{:S(2)}, u32[]{:S(2)}) %all-to-all-start.1) | async-done | bytes 1572896 | tf_op jit(solution)/shard_map/all_to_all | solution.py:89
  165.9 2.5 %copy.80 = bf16[16,4,6,2048]{3,2,1,0:T(8,128)(2,1)S(1)} copy(bf16[16,4,6,2048]{3,1,2,0:T(4,128)(2,1)} %all-to-all-done.1) | data formatting | bytes 3145728 | tf_op jit(solution)/shard_map/all_to_all | solution.py:89
  168.5 1.5 reshape.202
  169.9 2.0 %fusion.31 = f32[32,2048]{1,0:T(8,128)S(1)} fusion(bf16[384,2048,1]{1,0,2:T(8,128)(2,1)} %reshape.202, f32[32,6]{0,1:T(8,128)S(1)} %select_reduce_fusion, pred[32,6,384]{2,1,0:T(8,128)(4,1)S(1)} %and.29), kind=kOutput, calls=%fused_computation.27 | convolution fusion | flops 302710784 | bytes 1909504 | tf_op jit(solution)/shard_map/dot_general | solution.py:90
  171.9 12.5 %fusion.26 = bf16[32,2048]{1,0:T(8,128)(2,1)} fusion(f32[32,2048]{1,0:T(8,128)S(1)} %fusion.31, f32[32,2048]{1,0:T(8,128)S(1)} %get-tuple-element.16, bf16[2816,2048]{1,0:T(8,128)(2,1)} %param.36, bf16[2048,2816]{1,0:T(8,128)(2,1)} %param.35, f32[32,2816]{1,0:T(8,128)S(1)} %fusion.75, f32[2048]{0:T(1024)S(1)} %convert_element_type.102, f32[32]{0:T(128)S(1)} %add_rsqrt_fusion), kind=kOutput, calls=%fused_computation.21 | convolution fusion | flops 739131392 | bytes 24092800 | tf_op jit(solution)/shard_map/dot_general | solution.py:81
  (64 shorter events, 3.3 us)
Async XLA Ops:
  0.6 21.1 %copy-start = (bf16[2048,576]{0,1:T(8,128)(2,1)S(1)}, bf16[2048,576]{0,1:T(8,128)(2,1)}, u32[]{:S(2)}) copy-start(bf16[2048,576]{0,1:T(8,128)(2,1)} %param.29) | copy-start | bytes 7077892
  3.5 7.4 %copy-start.11 = (s32[32]{0:T(128)S(1)}, s32[32]{0:T(128)}, u32[]{:S(2)}) copy-start(s32[32]{0:T(128)} %param.23) | copy-start | bytes 388
  10.8 10.9 %copy-start.10 = (bf16[512]{0:T(512)(128)(2,1)S(1)}, bf16[512]{0:T(512)(128)(2,1)}, u32[]{:S(2)}) copy-start(bf16[512]{0:T(512)(128)(2,1)} %param.26) | copy-start | bytes 3076
  10.8 10.9 %copy-start.3 = (bf16[32,2048]{1,0:T(8,128)(2,1)S(1)}, bf16[32,2048]{1,0:T(8,128)(2,1)}, u32[]{:S(2)}) copy-start(bf16[32,2048]{1,0:T(8,128)(2,1)} %param.20) | copy-start | bytes 393220
  21.8 3.3 %copy-start.2 = (bf16[32,128,512]{2,1,0:T(8,128)(2,1)S(1)}, bf16[32,128,512]{2,1,0:T(8,128)(2,1)}, u32[]{:S(2)}) copy-start(bf16[32,128,512]{2,1,0:T(8,128)(2,1)} %param.21) | copy-start | bytes 12582916
  22.8 3.5 %copy-start.7 = (bf16[32,512]{1,0:T(8,128)(2,1)}, bf16[32,512]{1,0:T(8,128)(2,1)S(1)}, u32[]{:S(2)}) copy-start(bf16[32,512]{1,0:T(8,128)(2,1)S(1)} %get-tuple-element.4) | copy-start | bytes 98308
  25.1 5.7 %slice-start = ((s8[8388608]{0:T(1024)(128)(4,1)}), s8[4194304]{0:T(1024)(128)(4,1)S(1)}, s32[]{:S(2)}) async-start(s8[8388608]{0:T(1024)(128)(4,1)} %bitcast.81), calls=%async_computation.2 | async-start | bytes 8388608
  26.3 1.1 copy-start.5
  26.3 1.8 copy-start.9
  27.4 3.4 %slice-start.1 = ((s8[8388608]{0:T(1024)(128)(4,1)}), s8[4194304]{0:T(1024)(128)(4,1)S(1)}, s32[]{:S(2)}) async-start(s8[8388608]{0:T(1024)(128)(4,1)} %bitcast.81), calls=%async_computation.3 | async-start | bytes 8388608
  28.1 2.0 %copy-start.4 = (bf16[16,512,128]{2,1,0:T(8,128)(2,1)S(1)}, bf16[16,512,128]{2,1,0:T(8,128)(2,1)}, u32[]{:S(2)}) copy-start(bf16[16,512,128]{2,1,0:T(8,128)(2,1)} %param.31) | copy-start | bytes 6291460
  123.6 5.9 %copy-start.6 = (bf16[2048,64]{0,1:T(8,128)(2,1)S(1)}, bf16[2048,64]{0,1:T(8,128)(2,1)}, u32[]{:S(2)}) copy-start(bf16[2048,64]{0,1:T(8,128)(2,1)} %param.33) | copy-start | bytes 786436
  123.6 6.5 %copy-start.8 = (s32[32,6]{0,1:T(8,128)S(1)}, s32[32,6]{0,1:T(8,128)}, u32[]{:S(2)}) copy-start(s32[32,6]{0,1:T(8,128)} %param.24) | copy-start | bytes 2308
  123.6 42.3 %all-to-all-start.1 = ((bf16[16,4,6,2048]{3,1,2,0:T(4,128)(2,1)}), bf16[16,4,6,2048]{3,1,2,0:T(4,128)(2,1)}, u32[]{:S(2)}, u32[]{:S(2)}) async-start(bf16[16,4,6,2048]{3,1,2,0:T(4,128)(2,1)} %copy.79), calls=%async_computation.1 | async-start | bytes 3145728 | tf_op jit(solution)/shard_map/all_to_all | solution.py:89
  171.9 12.5 %copy-start.1 = (bf16[2048,576]{0,1:T(8,128)(2,1)S(1)}, bf16[2048,576]{0,1:T(8,128)(2,1)}, u32[]{:S(2)}) copy-start(bf16[2048,576]{0,1:T(8,128)(2,1)} %param.29) | copy-start | bytes 7077892
where the time goes:
time: 187 us; the launch traced here: 184 us
  matrix products  72.8 us (39%)
  blocking collectives  48.7 us (26%)
  waiting for transfers between devices  29.2 us (16%)
  local copies, waits for them, and re-layouts  18.4 us (10%)
  other arithmetic  9.2 us (5%)
  starting transfers between devices  5.18 us (3%)
    all_to_all x1, blocking collectives, moe_block(): recv_rows = lax.all_to_all(send_rows, 'dp', 0, 0, tiled=True)  48.7 us
    all_to_all x1, waiting for transfers between devices, moe_block(): lax.all_to_all(expert_rows, 'dp', 0, 0, tiled=True)  29.2 us
    dot_general x1, matrix products, moe_block(): jnp.einsum('secm,emf->secf', recv_rows, expert_up, preferred_element_type...  12.7 us
    dot_general x1, matrix products, moe_block(): jnp.dot(shared_act, shared_down, preferred_element_type=jnp.float32)  12.5 us
    dot_general x1, matrix products, moe_block(): jnp.einsum('secf,efm->secm', mid_act, expert_down, preferred_element_type...  11.5 us
    dot_general x1, matrix products, moe_block(): jnp.einsum('secm,emf->secf', recv_rows, expert_gate, preferred_element_ty...  10.1 us
    dot_general x1, matrix products, attention_block(): jnp.dot(normed_x, w_q, preferred_element_type=jnp.float32)  6.99 us
    dot_general x1, matrix products, moe_block(): jnp.dot(moe_in, shared_gate, preferred_element_type=jnp.float32)  6.41 us
  transfers between devices with their start and end apart: 1, of which 1 were waited for; matrix products, arithmetic and copies ran while one was open for 4% of the time, Pallas kernels for 0%

commit v1 on v0

v1 whole, which is shorter than its diff:
```python
import functools

import jax
import jax.numpy as jnp
from jax import lax
from jax.experimental import pallas as pl
from jax.experimental.pallas import tpu as pltpu
from jax.sharding import PartitionSpec as P

NORM_EPS = 1e-6
ROPE_THETA = 10000.0
MESH = pl.DeviceIdType.MESH


def rms_norm(values, gain_vec):
    vals_f32 = values.astype(jnp.float32)
    inv_rms = lax.rsqrt(jnp.mean(vals_f32 * vals_f32, axis=-1, keepdims=True) + NORM_EPS)
    return (vals_f32 * inv_rms * gain_vec.astype(jnp.float32)).astype(jnp.bfloat16)


def rope_tables(positions, rope_dim):
    inv_freq = ROPE_THETA ** (-2.0 * jnp.arange(rope_dim // 2, dtype=jnp.float32) / rope_dim)
    angles = positions.astype(jnp.float32)[:, None] * inv_freq[None, :]
    return jnp.cos(angles), jnp.sin(angles)


def apply_rope(values, rope_cos, rope_sin):
    half_dim = values.shape[-1] // 2
    first_half = values[..., :half_dim]
    second_half = values[..., half_dim:]
    return jnp.concatenate([first_half * rope_cos - second_half * rope_sin, second_half * rope_cos + first_half * rope_sin], axis=-1)


def attention_block(hidden, ckv_cache, kr_cache, seq_lens, attn_gain, kv_gain, w_q, w_dkv, w_uk, w_uv, w_o):
    batch_rows = hidden.shape[0]
    num_heads, nope_dim, value_a8 = w_uk.shape
    rope_dim = kr_cache.shape[-1]
    cache_len = ckv_cache.shape[1]
    score_scale = (nope_dim + rope_dim) ** -0.5
    normed_x = rms_norm(hidden, attn_gain)
    q_all = jnp.dot(normed_x, w_q, preferred_element_type=jnp.float32).astype(jnp.bfloat16).reshape(batch_rows, num_heads, nope_dim + rope_dim)
    latent_kv = jnp.dot(normed_x, w_dkv, preferred_element_type=jnp.float32)
    ckv_new = rms_norm(latent_kv[:, :value_a8], kv_gain)
    rope_cos, rope_sin = rope_tables(seq_lens, rope_dim)
    kr_new = apply_rope(latent_kv[:, value_a8:], rope_cos, rope_sin).astype(jnp.bfloat16)
    q_rot = apply_rope(q_all[:, :, nope_dim:].astype(jnp.float32), rope_cos[:, None, :], rope_sin[:, None, :]).astype(jnp.bfloat16)
    q_lat = jnp.einsum('bhn,hnc->bhc', q_all[:, :, :nope_dim], w_uk, preferred_element_type=jnp.float32).astype(jnp.bfloat16)
    scores = (jnp.einsum('bhc,blc->bhl', q_lat, ckv_cache, preferred_element_type=jnp.float32) + jnp.einsum('bhr,blr->bhl', q_rot, kr_cache, preferred_element_type=jnp.float32)) * score_scale
    valid_mask = jnp.arange(cache_len)[None, None, :] < seq_lens[:, None, None]
    scores = jnp.where(valid_mask, scores, -jnp.inf)
    new_score = (jnp.einsum('bhc,bc->bh', q_lat, ckv_new, preferred_element_type=jnp.float32) + jnp.einsum('bhr,br->bh', q_rot, kr_new, preferred_element_type=jnp.float32)) * score_scale
    top_score = jnp.maximum(jnp.max(scores, axis=-1), new_score)
    exp_cache = jnp.exp(scores - top_score[:, :, None])
    exp_new = jnp.exp(new_score - top_score)
    denominator = jnp.sum(exp_cache, axis=-1) + exp_new
    prob_cache = (exp_cache / denominator[:, :, None]).astype(jnp.bfloat16)
    prob_new = (exp_new / denominator).astype(jnp.bfloat16)
    o_lat = (jnp.einsum('bhl,blc->bhc', prob_cache, ckv_cache, preferred_element_type=jnp.float32) + jnp.einsum('bh,bc->bhc', prob_new, ckv_new, preferred_element_type=jnp.float32)).astype(jnp.bfloat16)
    head_out = jnp.einsum('bhc,hcv->bhv', o_lat, w_uv, preferred_element_type=jnp.float32).astype(jnp.bfloat16).reshape(batch_rows, -1)
    resid_out = (hidden.astype(jnp.float32) + jnp.dot(head_out, w_o, preferred_element_type=jnp.float32)).astype(jnp.bfloat16)
    return resid_out, ckv_new, kr_new


def moe_kernel(axis, topo, u_ref, g_ref, a_ref, sg_hbm, su_hbm, sd_hbm, eg_hbm, eu_hbm, ed_hbm, out_ref,
               u_all, g_all, x_buf, oht_buf, g_loc, acc_buf, mid_buf, y_buf, s_acc, part, px, ring_in,
               sgu_buf, sd_buf, gu_buf, dn_buf,
               sgu_sem, sd_sem, gu_sem, dn_sem,
               agu_send, agu_recv, agg_send, agg_recv, pru_send, pru_recv, prg_send, prg_recv,
               px_send, px_recv, rs_send, rs_recv):
    num_devs, half_steps = topo
    ring_len = num_devs // 2
    me = lax.axis_index(axis)
    ring_pos = me // 2
    core = me % 2
    up_dev = ((ring_pos + 1) % ring_len) * 2 + core
    down_dev = ((ring_pos + ring_len - 1) % ring_len) * 2 + core
    pair_dev = ring_pos * 2 + (1 - core)
    ring_dev = (up_dev, down_dev)
    rows, width = u_ref.shape
    half_rows = rows // 2
    local_experts, _, ff_dim = eg_hbm.shape
    shared_chunk = sd_buf.shape[1]
    num_shared = sd_hbm.shape[0] // shared_chunk
    shared_slots = sd_buf.shape[0]
    k_chunk = gu_buf.shape[1]
    num_k = width // k_chunk
    num_gu = local_experts * num_k
    gu_slots = gu_buf.shape[0]
    col_chunk = dn_buf.shape[2]
    num_cols = width // col_chunk
    num_dn = num_cols * local_experts
    dn_slots = dn_buf.shape[0]
    slots = x_buf.shape[1] // local_experts
    num_pieces = 2 * half_steps - 1

    def shared_copies(i):
        slot = lax.rem(i, shared_slots)
        off = pl.multiple_of(i * shared_chunk, shared_chunk)
        return (
            pltpu.make_async_copy(sg_hbm.at[:, pl.ds(off, shared_chunk)], sgu_buf.at[slot, :, pl.ds(0, shared_chunk)], sgu_sem.at[slot, 0]),
            pltpu.make_async_copy(su_hbm.at[:, pl.ds(off, shared_chunk)], sgu_buf.at[slot, :, pl.ds(shared_chunk, shared_chunk)], sgu_sem.at[slot, 1]),
            pltpu.make_async_copy(sd_hbm.at[pl.ds(off, shared_chunk), :], sd_buf.at[slot], sd_sem.at[slot]),
        )

    def gu_copies(j):
        slot = lax.rem(j, gu_slots)
        e = lax.div(j, num_k)
        off = pl.multiple_of(lax.rem(j, num_k) * k_chunk, k_chunk)
        return (
            pltpu.make_async_copy(eg_hbm.at[e, pl.ds(off, k_chunk), :], gu_buf.at[slot, :, pl.ds(0, ff_dim)], gu_sem.at[slot, 0]),
            pltpu.make_async_copy(eu_hbm.at[e, pl.ds(off, k_chunk), :], gu_buf.at[slot, :, pl.ds(ff_dim, ff_dim)], gu_sem.at[slot, 1]),
        )

    def dn_copy(q):
        slot = lax.rem(q, dn_slots)
        e = lax.rem(q, local_experts)
        off = pl.multiple_of(lax.div(q, local_experts) * col_chunk, col_chunk)
        return pltpu.make_async_copy(ed_hbm.at[e, :, pl.ds(off, col_chunk)], dn_buf.at[slot], dn_sem.at[slot])

    def start_all(copies):
        for cp in copies:
            cp.start()

    def wait_all(copies):
        for cp in copies:
            cp.wait()

    for i in range(min(shared_slots, num_shared)):
        start_all(shared_copies(i))

    barrier = pltpu.get_barrier_semaphore()
    for dev in (up_dev, down_dev, pair_dev):
        pl.semaphore_signal(barrier, inc=1, device_id={axis: dev}, device_id_type=MESH)
    pl.semaphore_wait(barrier, 3)

    def piece_rows(direction, p):
        half = lax.rem(p, 2)
        half = half if direction == 0 else 1 - half
        return pl.ds(pl.multiple_of(half * half_rows, half_rows), half_rows)

    def held_slot(direction, step):
        return lax.rem(ring_len - step, ring_len) if direction == 0 else step

    def gather_copies(direction, p, own):
        step = lax.div(p, 2)
        rws = piece_rows(direction, p)
        dst = held_slot(direction, step + 1)
        u_src = u_ref.at[rws] if own else u_all.at[0, held_slot(direction, step), rws]
        g_src = g_ref.at[rws] if own else g_all.at[0, held_slot(direction, step), rws]
        return (
            pltpu.make_async_remote_copy(src_ref=u_src, dst_ref=u_all.at[0, dst, rws], send_sem=agu_send.at[direction, p], recv_sem=agu_recv.at[direction, p], device_id={axis: ring_dev[direction]}, device_id_type=MESH),
            pltpu.make_async_remote_copy(src_ref=g_src, dst_ref=g_all.at[0, dst, rws], send_sem=agg_send.at[direction, p], recv_sem=agg_recv.at[direction, p], device_id={axis: ring_dev[direction]}, device_id_type=MESH),
        )

    def pair_copies(direction, p):
        rws = piece_rows(direction, p)
        slot = held_slot(direction, lax.div(p, 2) + 1)
        return (
            pltpu.make_async_remote_copy(src_ref=u_all.at[0, slot, rws], dst_ref=u_all.at[1, slot, rws], send_sem=pru_send.at[direction, p], recv_sem=pru_recv.at[direction, p], device_id={axis: pair_dev}, device_id_type=MESH),
            pltpu.make_async_remote_copy(src_ref=g_all.at[0, slot, rws], dst_ref=g_all.at[1, slot, rws], send_sem=prg_send.at[direction, p], recv_sem=prg_recv.at[direction, p], device_id={axis: pair_dev}, device_id_type=MESH),
        )

    pair_own = (
        pltpu.make_async_remote_copy(src_ref=u_ref, dst_ref=u_all.at[1, 0], send_sem=pru_send.at[0, num_pieces], recv_sem=pru_recv.at[0, num_pieces], device_id={axis: pair_dev}, device_id_type=MESH),
        pltpu.make_async_remote_copy(src_ref=g_ref, dst_ref=g_all.at[1, 0], send_sem=prg_send.at[0, num_pieces], recv_sem=prg_recv.at[0, num_pieces], device_id={axis: pair_dev}, device_id_type=MESH),
    )

    for p in range(2):
        for direction in range(2):
            start_all(gather_copies(direction, p, True))
    start_all(pair_own)
    u_all[0, 0] = u_ref[...]
    g_all[0, 0] = g_ref[...]

    def gather_event(p):
        for direction in range(2):
            for cp in gather_copies(direction, p, False):
                cp.wait_recv()

        @pl.when(p + 2 < num_pieces)
        def _():
            for direction in range(2):
                start_all(gather_copies(direction, p + 2, False))

        for direction in range(2):
            start_all(pair_copies(direction, p))

    s_acc[...] = jnp.zeros_like(s_acc)
    u_own = u_ref[...]

    def shared_step(i, carry):
        slot = lax.rem(i, shared_slots)
        wait_all(shared_copies(i))
        gu = jnp.dot(u_own, sgu_buf[slot], preferred_element_type=jnp.float32)
        act = (jax.nn.silu(gu[:, :shared_chunk]) * gu[:, shared_chunk:]).astype(jnp.bfloat16)
        s_acc[...] += jnp.dot(act, sd_buf[slot], preferred_element_type=jnp.float32)

        @pl.when(i + shared_slots < num_shared)
        def _():
            start_all(shared_copies(i + shared_slots))

        first_gu = num_shared - gu_slots

        @pl.when(i >= first_gu)
        def _():
            start_all(gu_copies(i - first_gu))

        turn = i - 2

        @pl.when((turn >= 0) & (lax.rem(turn + 3, 3) != 2))
        def _():
            gather_event(2 * lax.div(turn, 3) + lax.rem(turn, 3))

        return carry

    lax.fori_loop(0, num_shared, shared_step, 0)
    done_events = len([t for t in range(num_shared - 2) if t % 3 != 2])
    for p in range(done_events, num_pieces):
        gather_event(jnp.int32(p))
    for direction in range(2):
        for p in range(num_pieces):
            for cp in pair_copies(direction, p):
                cp.wait_recv()
    for cp in pair_own:
        cp.wait_recv()

    total_rows = num_devs * rows
    g_full = g_all[...].reshape(total_rows, g_all.shape[3])
    lanes = g_full.shape[1]
    g_mine = pltpu.roll(g_full, lax.rem(lanes - me * local_experts, lanes), 1)
    g_loc[...] = jnp.maximum(g_mine, 0.0)
    hit = g_mine >= 0.0
    row_i = lax.broadcasted_iota(jnp.int32, (total_rows, total_rows), 0)
    col_i = lax.broadcasted_iota(jnp.int32, (total_rows, total_rows), 1)
    before = jnp.where(col_i < row_i, 1.0, 0.0).astype(jnp.bfloat16)
    rank = jnp.dot(before, jnp.where(hit, 1.0, 0.0).astype(jnp.bfloat16), preferred_element_type=jnp.float32)
    place = jnp.where(hit, rank, -1.0)
    slot_i = lax.broadcasted_iota(jnp.int32, (total_rows, slots), 1).astype(jnp.float32)
    u_rows = u_all[...].reshape(total_rows, width)
    for e in range(local_experts):
        one_hot = jnp.where(slot_i == place[:, e:e + 1], 1.0, 0.0)
        oht_buf[e] = one_hot.astype(jnp.bfloat16)
        pick = one_hot.T.astype(jnp.bfloat16)
        for k in range(num_k):
            x_buf[k, e * slots:(e + 1) * slots] = jnp.dot(pick, u_rows[:, k * k_chunk:(k + 1) * k_chunk], preferred_element_type=jnp.float32).astype(jnp.bfloat16)

    def expert_step(e, carry):
        for k in range(num_k):
            j = e * num_k + k
            slot = lax.rem(j, gu_slots)
            wait_all(gu_copies(j))
            prod = jnp.dot(x_buf[k, pl.ds(pl.multiple_of(e * slots, slots), slots)], gu_buf[slot], preferred_element_type=jnp.float32)
            if k == 0:
                acc_buf[...] = prod
            else:
                acc_buf[...] += prod

            @pl.when(j + gu_slots < num_gu)
            def _():
                start_all(gu_copies(j + gu_slots))

            @pl.when((j + gu_slots >= num_gu) & (j + gu_slots - num_gu < dn_slots))
            def _():
                dn_copy(j + gu_slots - num_gu).start()

        mid_buf[e] = (jax.nn.silu(acc_buf[:, :ff_dim]) * acc_buf[:, ff_dim:]).astype(jnp.bfloat16)
        return carry

    lax.fori_loop(0, local_experts, expert_step, 0)
    for q in range(min(gu_slots, dn_slots), min(dn_slots, num_dn)):
        dn_copy(q).start()

    half_cols = col_chunk // 2

    def pair_sum_copy(c):
        return pltpu.make_async_remote_copy(src_ref=part.at[c, 1], dst_ref=px.at[c], send_sem=px_send.at[c], recv_sem=px_recv.at[c], device_id={axis: pair_dev}, device_id_type=MESH)

    def sum_slot(direction, step):
        return half_steps - step if direction == 0 else (half_steps + step) % ring_len

    def ring_copy(c, direction, step):
        slot = sum_slot(direction, step)
        if step == 0:
            cols = pl.ds(direction * half_cols, half_cols)
            src, dst = part.at[c, 0, slot, :, cols], ring_in.at[direction, c, step, :, cols]
        else:
            src, dst = part.at[c, 0, slot], ring_in.at[direction, c, step]
        return pltpu.make_async_remote_copy(src_ref=src, dst_ref=dst, send_sem=rs_send.at[direction, c, step], recv_sem=rs_recv.at[direction, c, step], device_id={axis: ring_dev[direction]}, device_id_type=MESH)

    def column_sums(c):
        def down_step(e, carry):
            q = c * local_experts + e
            slot = lax.rem(q, dn_slots)
            dn_copy(q).wait()
            y_buf[e] = jnp.dot(mid_buf[e], dn_buf[slot], preferred_element_type=jnp.float32).astype(jnp.bfloat16)

            @pl.when(q + dn_slots < num_dn)
            def _():
                dn_copy(q + dn_slots).start()

            return carry

        lax.fori_loop(0, local_experts, down_step, 0)
        total = None
        for e in range(local_experts):
            spread = jnp.dot(oht_buf[e], y_buf[e], preferred_element_type=jnp.float32) * g_loc[:, e:e + 1]
            total = spread if total is None else total + spread
        part[c] = total.reshape(2, ring_len, rows, col_chunk)
        pair_sum_copy(c).start()

    def ring_step(c, step):
        if step == 0:
            pair_sum_copy(c).wait_recv()
            part[c, 0, half_steps] += px[c, half_steps]
            for direction in range(2):
                ring_copy(c, direction, 0).start()
            return
        for direction in range(2):
            slot = sum_slot(direction, step)
            ring_copy(c, direction, step - 1).wait_recv()
            if step == 1:
                cols = slice(direction * half_cols, (direction + 1) * half_cols)
                part[c, 0, slot] += px[c, slot]
                part[c, 0, slot, :, cols] += ring_in[direction, c, 0, :, cols]
            elif step < half_steps:
                part[c, 0, slot] += px[c, slot] + ring_in[direction, c, step - 1]
            if step < half_steps:
                ring_copy(c, direction, step).start()
        if step == half_steps:
            cols = slice(c * col_chunk, (c + 1) * col_chunk)
            routed = part[c, 0, 0] + px[c, 0] + ring_in[0, c, step - 1] + ring_in[1, c, step - 1]
            out_ref[:, cols] = (a_ref[:, cols].astype(jnp.float32) + s_acc[:, cols] + routed).astype(jnp.bfloat16)

    for turn in range(num_cols + half_steps + 1):
        if turn < num_cols:
            column_sums(turn)
        for step in range(half_steps + 1):
            c = turn - 1 - step
            if 0 <= c < num_cols:
                ring_step(c, step)

    for direction in range(2):
        for p in range(num_pieces):
            for cp in gather_copies(direction, p, p < 2) + pair_copies(direction, p):
                cp.wait_send()
        for c in range(num_cols):
            for step in range(half_steps):
                ring_copy(c, direction, step).wait_send()
    for cp in pair_own:
        cp.wait_send()
    for c in range(num_cols):
        pair_sum_copy(c).wait_send()


def moe_call(axis, num_devs, moe_in, gate_rows, resid_out, shared_gate, shared_up, shared_down, expert_gate, expert_up, expert_down, slots):
    rows, width = moe_in.shape
    local_experts, _, ff_dim = expert_gate.shape
    shared_dim = shared_down.shape[0]
    ring_len = num_devs // 2
    half_steps = ring_len // 2
    shared_chunk = 256
    shared_slots = 3
    k_chunk = min(512, width // 2)
    num_k = width // k_chunk
    gu_slots = min(6, shared_dim // shared_chunk, local_experts * num_k)
    num_cols = 4
    col_chunk = width // num_cols
    dn_slots = 8
    num_pieces = 2 * half_steps - 1
    lanes = gate_rows.shape[1]
    f32, bf16 = jnp.float32, jnp.bfloat16
    vmem = pl.BlockSpec(memory_space=pltpu.VMEM)
    anym = pl.BlockSpec(memory_space=pl.ANY)
    dma = pltpu.SemaphoreType.DMA
    return pl.pallas_call(
        functools.partial(moe_kernel, axis, (num_devs, half_steps)),
        name='moe_ring',
        out_shape=jax.ShapeDtypeStruct((rows, width), bf16),
        in_specs=[vmem] * 3 + [anym] * 6,
        out_specs=vmem,
        scratch_shapes=[
            pltpu.VMEM((2, ring_len, rows, width), bf16),
            pltpu.VMEM((2, ring_len, rows, lanes), f32),
            pltpu.VMEM((num_k, local_experts * slots, k_chunk), bf16),
            pltpu.VMEM((local_experts, num_devs * rows, slots), bf16),
            pltpu.VMEM((num_devs * rows, lanes), f32),
            pltpu.VMEM((slots, 2 * ff_dim), f32),
            pltpu.VMEM((local_experts, slots, ff_dim), bf16),
            pltpu.VMEM((local_experts, slots, col_chunk), bf16),
            pltpu.VMEM((rows, width), f32),
            pltpu.VMEM((num_cols, 2, ring_len, rows, col_chunk), f32),
            pltpu.VMEM((num_cols, ring_len, rows, col_chunk), f32),
            pltpu.VMEM((2, num_cols, half_steps, rows, col_chunk), f32),
            pltpu.VMEM((shared_slots, width, 2 * shared_chunk), bf16),
            pltpu.VMEM((shared_slots, shared_chunk, width), bf16),
            pltpu.VMEM((gu_slots, k_chunk, 2 * ff_dim), bf16),
            pltpu.VMEM((dn_slots, ff_dim, col_chunk), bf16),
            dma((shared_slots, 2)), dma((shared_slots,)), dma((gu_slots, 2)), dma((dn_slots,)),
            dma((2, num_pieces)), dma((2, num_pieces)), dma((2, num_pieces)), dma((2, num_pieces)),
            dma((2, num_pieces + 1)), dma((2, num_pieces + 1)), dma((2, num_pieces + 1)), dma((2, num_pieces + 1)),
            dma((num_cols,)), dma((num_cols,)), dma((2, num_cols, half_steps)), dma((2, num_cols, half_steps)),
        ],
        compiler_params=pltpu.CompilerParams(collective_id=0, has_side_effects=True, vmem_limit_bytes=67043328),
    )(moe_in, gate_rows, resid_out, shared_gate, shared_up, shared_down, expert_gate, expert_up, expert_down)


def gate_table(moe_in, expert_ids, w_router, lanes):
    num_experts = w_router.shape[1]
    router_prob = jax.nn.softmax(jnp.dot(moe_in, w_router, preferred_element_type=jnp.float32), axis=-1)
    picked = jnp.any(expert_ids[:, :, None] == jnp.arange(num_experts)[None, None, :], axis=1)
    return jnp.pad(jnp.where(picked, router_prob, -1.0), ((0, 0), (0, lanes - num_experts)), constant_values=-1.0)


def solution(mesh):
    row_spec = P(('rep', 'dp'))
    full_spec = P()
    expert_spec = P('dp')
    num_devs = mesh.shape['dp']

    def device_step(hidden, ckv_cache, kr_cache, seq_lens, expert_ids, attn_gain, kv_gain, moe_gain, w_q, w_dkv, w_uk, w_uv, w_o, w_router, shared_gate, shared_up, shared_down, expert_gate, expert_up, expert_down):
        num_experts = w_router.shape[1]
        capacity = max(2, 2 * hidden.shape[0] * expert_ids.shape[1] // num_experts)
        slots = -(-capacity * num_devs // 128) * 128
        lanes = -(-num_experts // 128) * 128
        resid_out, ckv_new, kr_new = attention_block(hidden, ckv_cache, kr_cache, seq_lens, attn_gain, kv_gain, w_q, w_dkv, w_uk, w_uv, w_o)
        moe_in = rms_norm(resid_out, moe_gain)
        gate_rows = gate_table(moe_in, expert_ids, w_router, lanes)
        layer_out = moe_call('dp', num_devs, moe_in, gate_rows, resid_out, shared_gate, shared_up, shared_down, expert_gate, expert_up, expert_down, slots)
        return layer_out, ckv_new, kr_new

    in_specs = (row_spec,) * 5 + (full_spec,) * 12 + (expert_spec,) * 3
    return jax.shard_map(device_step, mesh=mesh, in_specs=in_specs, out_specs=(row_spec, row_spec, row_spec), check_vma=False)
```

time: 187 us -> 98.7 us (0.53); the launches traced: 184 us -> 98.5 us
  Pallas kernels: 0 us -> 70.9 us
  matrix products: 72.8 us -> 15.6 us
  blocking collectives: 48.7 us -> 0 us
  waiting for transfers between devices: 29.2 us -> 0 us
  local copies, waits for them, and re-layouts: 18.4 us -> 5.71 us
  starting transfers between devices: 5.18 us -> 0 us
  other arithmetic: 9.2 us -> 5.28 us
    pallas_call x0 -> x1, Pallas kernels: none -> 70.9 us  [moe_call(): pl.pallas_call(functools.partial(moe_kernel, axis, (num_devs, half_steps)...]
    dot_general x8 -> x1, matrix products: 57.4 us -> 0.3 us  [gate_table(): jnp.dot(moe_in, w_router, preferred_element_type=jnp.float32)]
    all_to_all x1 -> x0, blocking collectives: 48.7 us -> none  [moe_block(): recv_rows = lax.all_to_all(send_rows, 'dp', 0, 0, tiled=True)]
    all_to_all x1 -> x0, waiting for transfers between devices: 29.2 us -> none  [moe_block(): lax.all_to_all(expert_rows, 'dp', 0, 0, tiled=True)]
    reshape x3 -> x0, local copies, waits for them, and re-layouts: 5.28 us -> none  [the longest x2 3.83 us: moe_block(): jnp.einsum('tx,tm->xm', dispatch, moe_in, preferred_element_type=jnp.floa...]
    and x1 -> x0, local copies, waits for them, and re-layouts: 5.26 us -> none  [route_tables(): pick_flat[:, :, None] & slot_hit[:, None, :]]
    all_to_all x1 -> x0, starting transfers between devices: 5.18 us -> none  [moe_block(): lax.all_to_all(expert_rows, 'dp', 0, 0, tiled=True)]
    and x1 -> x0, other arithmetic: 4.11 us -> none  [route_tables(): pick_flat[:, :, None] & slot_hit[:, None, :]]
  transfers between devices with their start and end apart: 1 -> 0, of which waited for: 1 -> 0; matrix products, arithmetic and copies ran while one was open for 4% -> 0% of each run, Pallas kernels for 0% -> 0%
where the time goes in v1:
time: 98.7 us; the launch traced here: 98.5 us
  Pallas kernels  70.9 us (72%)
  matrix products  15.6 us (16%)
  local copies, waits for them, and re-layouts  5.71 us (6%)
  other arithmetic  5.28 us (5%)
    pallas_call x1, Pallas kernels, moe_call(): pl.pallas_call(functools.partial(moe_kernel, axis, (num_devs, half_steps)...  70.9 us
    dot_general x1, matrix products, attention_block(): jnp.dot(normed_x, w_q, preferred_element_type=jnp.float32)  7.11 us
    unnamed x35, local copies, waits for them, and re-layouts  4.77 us
    dot_general x1, matrix products, attention_block(): latent_kv = jnp.dot(normed_x, w_dkv, preferred_element_type=jnp.float32)  2.54 us

profile of v1, /device:TPU:22, one launch (start us, length us, event | category | flops | bytes accessed | tf_op | source)
XLA Modules:
  0.0 98.5 jit_solution(15363157518850562231)
XLA Ops:
  0.6 0.7 convert_element_type.61
  1.3 1.0 %fusion.14 = f32[32]{0:T(128)S(1)} fusion(bf16[32,2048]{1,0:T(8,128)(2,1)} %param.20), kind=kLoop, calls=%fused_computation.24 | loop fusion | flops 196576 | bytes 131200 | tf_op jit(solution)/shard_map/reduce_sum | solution.py:17
  2.4 2.5 %fusion.25 = f32[32,576]{1,0:T(8,128)S(1)} fusion(bf16[2048,576]{0,1:T(8,128)(2,1)} %param.29, bf16[32,2048]{1,0:T(8,128)(2,1)} %param.20, f32[2048]{0:T(1024)S(1)} %convert_element_type.61, f32[32]{0:T(128)S(1)} %add_rsqrt_fusion.2), kind=kOutput, calls=%fused_computation.44 | convolution fusion | flops 75759616 | bytes 2572416 | tf_op jit(solution)/shard_map/dot_general | solution.py:42
  4.9 0.7 convert_element_type.67
  5.6 0.1 subtract_convert_fusion.1
  5.8 7.1 %convolution_convert_fusion = bf16[32,3072]{1,0:T(8,128)(2,1)S(1)} fusion(bf16[2048,3072]{1,0:T(8,128)(2,1)} %param.28, bf16[32,2048]{1,0:T(8,128)(2,1)} %param.20, f32[2048]{0:T(1024)S(1)} %convert_element_type.61, f32[32]{0:T(128)S(1)} %add_rsqrt_fusion.2), kind=kOutput, calls=%fused_computation | convolution fusion | flops 403013632 | bytes 12918912 | tf_op jit(solution)/shard_map/dot_general | solution.py:41
  12.9 0.3 reshape.115
  13.2 0.2 subtract_convert_fusion
  13.6 0.2 fusion.28
  13.9 0.4 fusion.2
  14.3 1.1 %copy-done = bf16[32,128,512]{2,1,0:T(8,128)(2,1)S(1)} copy-done((bf16[32,128,512]{2,1,0:T(8,128)(2,1)S(1)}, bf16[32,128,512]{2,1,0:T(8,128)(2,1)}, u32[]{:S(2)}) %copy-start) | copy-done | bytes 4194328
  15.4 1.2 %fusion.9 = f32[32,16,128]{2,1,0:T(8,128)S(1)} fusion(bf16[32,128,512]{2,1,0:T(8,128)(2,1)S(1)} %copy-done, bf16[32,16,512]{2,0,1:T(8,128)(2,1)S(1)} %fusion.2), kind=kOutput, calls=%fused_computation.15 | convolution fusion | flops 67108864 | bytes 4980736 | tf_op jit(solution)/shard_map/bhc,blc->bhl/dot_general | solution.py:48
  16.6 0.1 iota_compare_fusion.1
  16.7 0.4 fusion.37
  17.1 0.1 multiply_reduce_fusion
  17.3 0.4 fusion.7
  17.7 0.2 copy-done.10
  17.9 0.2 fusion.17
  18.2 0.7 fusion.1
  19.0 0.6 fusion.5
  19.6 0.6 slice-done.1
  20.2 1.7 %fusion.11 = (f32[32]{0:T(128)S(1)}, bf16[32,2048]{1,0:T(8,128)(2,1)S(1)}) fusion(bf16[2048,2048]{1,0:T(8,128)(2,1)S(1)} %bitcast.28, bf16[16,4,8,128]{3,2,1,0:T(8,128)(2,1)S(1)} %fusion.5, bf16[32,2048]{1,0:T(8,128)(2,1)S(1)} %copy-done.1), kind=kOutput, calls=%fused_computation.21 | convolution fusion | flops 268828640 | bytes 8781952 | tf_op jit(solution)/shard_map/dot_general | solution.py:60
  21.9 0.6 copy-done.4
  22.5 0.1 fusion.13.u_ref
  22.6 0.6 copy-done.5
  23.2 0.3 fusion.38
  23.6 0.2 fusion.30
  23.8 0.1 fusion.23
  23.9 0.6 pad.4.g_ref
  24.6 70.9 %moe_ring.1 = bf16[32,2048]{1,0:T(8,128)(2,1)} custom-call(bf16[32,2048]{1,0:T(8,128)(2,1)} %copy-done.5, f32[32,128]{1,0:T(8,128)} %pad.4.g_ref, bf16[32,2048]{1,0:T(8,128)(2,1)} %copy-done.4, bf16[2048,2816]{1,0:T(8,128)(2,1)} %sg_hbm.1, bf16[2048,2816]{1,0:T(8,128)(2,1)} %su_hbm.1, bf16[2816,2048]{1,0:T(8,128)(2,1)} %sd_hbm.1, ...), custom_call_target="tpu_custom_call" | custom-call | tf_op jit(solution)/shard_map/moe_ring/pallas_call | solution.py:375
  95.5 1.4 %pad_maximum_fusion.3 = bf16[32,64]{1,0:T(8,128)(2,1)} fusion(bf16[32,32]{1,0:T(8,128)(2,1)} %copy-done.9, bf16[32,32]{1,0:T(8,128)(2,1)} %copy-done.8), kind=kLoop, calls=%fused_computation.59 | loop fusion | flops 8192 | bytes 8192 | tf_op jit(solution)/shard_map/concatenate | solution.py:31
  96.9 1.6 %copy.61 = bf16[32,2048]{1,0:T(8,128)(2,1)} copy(bf16[32,2048]{1,0:T(8,128)(2,1)} %moe_ring.1) | data formatting | bytes 262144
  (43 shorter events, 0.4 us)
Async XLA Ops:
  5.7 7.7 %copy-start.8 = (bf16[32,32]{1,0:T(8,128)(2,1)}, bf16[32,32]{1,0:T(8,128)(2,1)S(1)}, u32[]{:S(2)}) copy-start(bf16[32,32]{1,0:T(8,128)(2,1)S(1)} %get-tuple-element.7) | copy-start | bytes 6148
  5.8 7.7 %copy-start.9 = (bf16[32,32]{1,0:T(8,128)(2,1)}, bf16[32,32]{1,0:T(8,128)(2,1)S(1)}, u32[]{:S(2)}) copy-start(bf16[32,32]{1,0:T(8,128)(2,1)S(1)} %get-tuple-element.8) | copy-start | bytes 6148
  5.8 8.1 %copy-start.2 = (bf16[16,128,512]{2,1,0:T(8,128)(2,1)S(1)}, bf16[16,128,512]{2,1,0:T(8,128)(2,1)}, u32[]{:S(2)}) copy-start(bf16[16,128,512]{2,1,0:T(8,128)(2,1)} %param.30) | copy-start | bytes 6291460
  13.2 2.2 %copy-start = (bf16[32,128,512]{2,1,0:T(8,128)(2,1)S(1)}, bf16[32,128,512]{2,1,0:T(8,128)(2,1)}, u32[]{:S(2)}) copy-start(bf16[32,128,512]{2,1,0:T(8,128)(2,1)} %param.21) | copy-start | bytes 12582916
  13.4 3.2 %copy-start.14 = (s32[32]{0:T(128)S(1)}, s32[32]{0:T(128)}, u32[]{:S(2)}) copy-start(s32[32]{0:T(128)} %param.23) | copy-start | bytes 388
  13.4 3.2 %copy-start.6 = (bf16[32,128,64]{1,2,0:T(8,128)(2,1)S(1)}, bf16[32,128,64]{1,2,0:T(8,128)(2,1)}, u32[]{:S(2)}) copy-start(bf16[32,128,64]{1,2,0:T(8,128)(2,1)} %param.22) | copy-start | bytes 1572868
  13.9 3.4 %copy-start.13 = (bf16[512]{0:T(512)(128)(2,1)S(1)}, bf16[512]{0:T(512)(128)(2,1)}, u32[]{:S(2)}) copy-start(bf16[512]{0:T(512)(128)(2,1)} %param.26) | copy-start | bytes 3076
  15.4 4.2 %slice-start = ((s8[8388608]{0:T(1024)(128)(4,1)}), s8[4194304]{0:T(1024)(128)(4,1)S(1)}, s32[]{:S(2)}) async-start(s8[8388608]{0:T(1024)(128)(4,1)} %bitcast.27), calls=%async_computation | async-start | bytes 8388608
  16.6 2.4 %copy-start.3 = (bf16[16,512,128]{2,1,0:T(8,128)(2,1)S(1)}, bf16[16,512,128]{2,1,0:T(8,128)(2,1)}, u32[]{:S(2)}) copy-start(bf16[16,512,128]{2,1,0:T(8,128)(2,1)} %param.31) | copy-start | bytes 6291460
  17.3 0.6 copy-start.10
  17.7 1.9 %copy-start.1 = (bf16[32,2048]{1,0:T(8,128)(2,1)S(1)}, bf16[32,2048]{1,0:T(8,128)(2,1)}, u32[]{:S(2)}) copy-start(bf16[32,2048]{1,0:T(8,128)(2,1)} %param.20) | copy-start | bytes 393220
  17.9 2.2 %slice-start.1 = ((s8[8388608]{0:T(1024)(128)(4,1)}), s8[4194304]{0:T(1024)(128)(4,1)S(1)}, s32[]{:S(2)}) async-start(s8[8388608]{0:T(1024)(128)(4,1)} %bitcast.27), calls=%async_computation.1 | async-start | bytes 8388608
  20.2 1.7 %copy-start.11 = (bf16[2048]{0:T(1024)(128)(2,1)S(1)}, bf16[2048]{0:T(1024)(128)(2,1)}, u32[]{:S(2)}) copy-start(bf16[2048]{0:T(1024)(128)(2,1)} %param.27) | copy-start | bytes 12292
  20.2 3.1 %copy-start.7 = (bf16[2048,64]{0,1:T(8,128)(2,1)S(1)}, bf16[2048,64]{0,1:T(8,128)(2,1)}, u32[]{:S(2)}) copy-start(bf16[2048,64]{0,1:T(8,128)(2,1)} %param.33) | copy-start | bytes 786436
  20.2 3.6 %copy-start.12 = (s32[32,6]{0,1:T(8,128)S(1)}, s32[32,6]{0,1:T(8,128)}, u32[]{:S(2)}) copy-start(s32[32,6]{0,1:T(8,128)} %param.24) | copy-start | bytes 2308
  21.8 0.7 copy-start.4
  22.6 0.7 copy-start.5

commit v2 on v1

--- a/solution.py
+++ b/solution.py
@@ -62,9 +62,8 @@
 
 
 def moe_kernel(axis, topo, u_ref, g_ref, a_ref, sg_hbm, su_hbm, sd_hbm, eg_hbm, eu_hbm, ed_hbm, out_ref,
-               u_all, g_all, x_buf, oht_buf, g_loc, acc_buf, mid_buf, y_buf, s_acc, part, px, ring_in,
-               sgu_buf, sd_buf, gu_buf, dn_buf,
-               sgu_sem, sd_sem, gu_sem, dn_sem,
+               u_all, g_all, x_buf, oht_buf, g_loc, acc_buf, mid_buf, shared_mid, y_buf, s_acc, part, px, ring_in,
+               gu_buf, dn_buf, gu_sem, dn_sem,
                agu_send, agu_recv, agg_send, agg_recv, pru_send, pru_recv, prg_send, prg_recv,
                px_send, px_recv, rs_send, rs_recv):
     num_devs, half_steps = topo
@@ -79,9 +78,6 @@
     rows, width = u_ref.shape
     half_rows = rows // 2
     local_experts, _, ff_dim = eg_hbm.shape
-    shared_chunk = sd_buf.shape[1]
-    num_shared = sd_hbm.shape[0] // shared_chunk
-    shared_slots = sd_buf.shape[0]
     k_chunk = gu_buf.shape[1]
     num_k = width // k_chunk
     num_gu = local_experts * num_k
@@ -91,16 +87,9 @@
     num_dn = num_cols * local_experts
     dn_slots = dn_buf.shape[0]
     slots = x_buf.shape[1] // local_experts
+    num_shared_gu = 2 * num_k
+    num_shared_dn = 2 * num_cols
     num_pieces = 2 * half_steps - 1
-
-    def shared_copies(i):
-        slot = lax.rem(i, shared_slots)
-        off = pl.multiple_of(i * shared_chunk, shared_chunk)
-        return (
-            pltpu.make_async_copy(sg_hbm.at[:, pl.ds(off, shared_chunk)], sgu_buf.at[slot, :, pl.ds(0, shared_chunk)], sgu_sem.at[slot, 0]),
-            pltpu.make_async_copy(su_hbm.at[:, pl.ds(off, shared_chunk)], sgu_buf.at[slot, :, pl.ds(shared_chunk, shared_chunk)], sgu_sem.at[slot, 1]),
-            pltpu.make_async_copy(sd_hbm.at[pl.ds(off, shared_chunk), :], sd_buf.at[slot], sd_sem.at[slot]),
-        )
 
     def gu_copies(j):
         slot = lax.rem(j, gu_slots)
@@ -111,6 +100,16 @@
             pltpu.make_async_copy(eu_hbm.at[e, pl.ds(off, k_chunk), :], gu_buf.at[slot, :, pl.ds(ff_dim, ff_dim)], gu_sem.at[slot, 1]),
         )
 
+    def shared_gu_copy(j):
+        src = (sg_hbm, su_hbm)[j // num_k]
+        slot = (num_gu + j) % gu_slots
+        return pltpu.make_async_copy(src.at[pl.ds((j % num_k) * k_chunk, k_chunk), :], gu_buf.at[slot], gu_sem.at[slot, 0])
+
+    def shared_dn_copy(q):
+        slot = (num_dn + q) % dn_slots
+        rws = pl.ds((q % 2) * ff_dim, ff_dim)
+        return pltpu.make_async_copy(sd_hbm.at[rws, pl.ds((q // 2) * col_chunk, col_chunk)], dn_buf.at[slot], dn_sem.at[slot])
+
     def dn_copy(q):
         slot = lax.rem(q, dn_slots)
         e = lax.rem(q, local_experts)
@@ -125,8 +124,10 @@
         for cp in copies:
             cp.wait()
 
-    for i in range(min(shared_slots, num_shared)):
-        start_all(shared_copies(i))
+    for j in range(gu_slots):
+        start_all(gu_copies(j))
+    for q in range(dn_slots):
+        dn_copy(q).start()
 
     barrier = pltpu.get_barrier_semaphore()
     for dev in (up_dev, down_dev, pair_dev):
@@ -134,15 +135,14 @@
     pl.semaphore_wait(barrier, 3)
 
     def piece_rows(direction, p):
-        half = lax.rem(p, 2)
-        half = half if direction == 0 else 1 - half
-        return pl.ds(pl.multiple_of(half * half_rows, half_rows), half_rows)
+        half = p % 2 if direction == 0 else 1 - p % 2
+        return pl.ds(half * half_rows, half_rows)
 
     def held_slot(direction, step):
-        return lax.rem(ring_len - step, ring_len) if direction == 0 else step
+        return (ring_len - step) % ring_len if direction == 0 else step
 
     def gather_copies(direction, p, own):
-        step = lax.div(p, 2)
+        step = p // 2
         rws = piece_rows(direction, p)
         dst = held_slot(direction, step + 1)
         u_src = u_ref.at[rws] if own else u_all.at[0, held_slot(direction, step), rws]
@@ -154,7 +154,7 @@
 
     def pair_copies(direction, p):
         rws = piece_rows(direction, p)
-        slot = held_slot(direction, lax.div(p, 2) + 1)
+        slot = held_slot(direction, p // 2 + 1)
         return (
             pltpu.make_async_remote_copy(src_ref=u_all.at[0, slot, rws], dst_ref=u_all.at[1, slot, rws], send_sem=pru_send.at[direction, p], recv_sem=pru_recv.at[direction, p], device_id={axis: pair_dev}, device_id_type=MESH),
             pltpu.make_async_remote_copy(src_ref=g_all.at[0, slot, rws], dst_ref=g_all.at[1, slot, rws], send_sem=prg_send.at[direction, p], recv_sem=prg_recv.at[direction, p], device_id={axis: pair_dev}, device_id_type=MESH),
@@ -177,46 +177,14 @@
             for cp in gather_copies(direction, p, False):
                 cp.wait_recv()
 
-        @pl.when(p + 2 < num_pieces)
-        def _():
+        if p + 2 < num_pieces:
             for direction in range(2):
                 start_all(gather_copies(direction, p + 2, False))
-
         for direction in range(2):
             start_all(pair_copies(direction, p))
 
-    s_acc[...] = jnp.zeros_like(s_acc)
-    u_own = u_ref[...]
-
-    def shared_step(i, carry):
-        slot = lax.rem(i, shared_slots)
-        wait_all(shared_copies(i))
-        gu = jnp.dot(u_own, sgu_buf[slot], preferred_element_type=jnp.float32)
-        act = (jax.nn.silu(gu[:, :shared_chunk]) * gu[:, shared_chunk:]).astype(jnp.bfloat16)
-        s_acc[...] += jnp.dot(act, sd_buf[slot], preferred_element_type=jnp.float32)
-
-        @pl.when(i + shared_slots < num_shared)
-        def _():
-            start_all(shared_copies(i + shared_slots))
-
-        first_gu = num_shared - gu_slots
-
-        @pl.when(i >= first_gu)
-        def _():
-            start_all(gu_copies(i - first_gu))
-
-        turn = i - 2
-
-        @pl.when((turn >= 0) & (lax.rem(turn + 3, 3) != 2))
-        def _():
-            gather_event(2 * lax.div(turn, 3) + lax.rem(turn, 3))
-
-        return carry
-
-    lax.fori_loop(0, num_shared, shared_step, 0)
-    done_events = len([t for t in range(num_shared - 2) if t % 3 != 2])
-    for p in range(done_events, num_pieces):
-        gather_event(jnp.int32(p))
+    for p in range(num_pieces):
+        gather_event(p)
     for direction in range(2):
         for p in range(num_pieces):
             for cp in pair_copies(direction, p):
@@ -259,17 +227,10 @@
             def _():
                 start_all(gu_copies(j + gu_slots))
 
-            @pl.when((j + gu_slots >= num_gu) & (j + gu_slots - num_gu < dn_slots))
-            def _():
-                dn_copy(j + gu_slots - num_gu).start()
-
         mid_buf[e] = (jax.nn.silu(acc_buf[:, :ff_dim]) * acc_buf[:, ff_dim:]).astype(jnp.bfloat16)
         return carry
 
     lax.fori_loop(0, local_experts, expert_step, 0)
-    for q in range(min(gu_slots, dn_slots), min(dn_slots, num_dn)):
-        dn_copy(q).start()
-
     half_cols = col_chunk // 2
 
     def pair_sum_copy(c):
@@ -288,19 +249,18 @@
         return pltpu.make_async_remote_copy(src_ref=src, dst_ref=dst, send_sem=rs_send.at[direction, c, step], recv_sem=rs_recv.at[direction, c, step], device_id={axis: ring_dev[direction]}, device_id_type=MESH)
 
     def column_sums(c):
-        def down_step(e, carry):
+        for e in range(local_experts):
             q = c * local_experts + e
-            slot = lax.rem(q, dn_slots)
             dn_copy(q).wait()
-            y_buf[e] = jnp.dot(mid_buf[e], dn_buf[slot], preferred_element_type=jnp.float32).astype(jnp.bfloat16)
-
-            @pl.when(q + dn_slots < num_dn)
-            def _():
-                dn_copy(q + dn_slots).start()
-
-            return carry
-
-        lax.fori_loop(0, local_experts, down_step, 0)
+            y_buf[e] = jnp.dot(mid_buf[e], dn_buf[q % dn_slots], preferred_element_type=jnp.float32).astype(jnp.bfloat16)
+            ahead = q + dn_slots
+            if ahead < num_dn:
+                dn_copy(ahead).start()
+            else:
+                if ahead - num_dn < num_shared_gu:
+                    shared_gu_copy(ahead - num_dn).start()
+                if ahead - num_dn < num_shared_dn:
+                    shared_dn_copy(ahead - num_dn).start()
         total = None
         for e in range(local_experts):
             spread = jnp.dot(oht_buf[e], y_buf[e], preferred_element_type=jnp.float32) * g_loc[:, e:e + 1]
@@ -327,9 +287,32 @@
             if step < half_steps:
                 ring_copy(c, direction, step).start()
         if step == half_steps:
-            cols = slice(c * col_chunk, (c + 1) * col_chunk)
-            routed = part[c, 0, 0] + px[c, 0] + ring_in[0, c, step - 1] + ring_in[1, c, step - 1]
-            out_ref[:, cols] = (a_ref[:, cols].astype(jnp.float32) + s_acc[:, cols] + routed).astype(jnp.bfloat16)
+            part[c, 0, 0] += px[c, 0] + ring_in[0, c, step - 1] + ring_in[1, c, step - 1]
+
+    def shared_gu(j):
+        shared_gu_copy(j).wait()
+        k = j % num_k
+        rws = pl.ds((j // num_k) * rows, rows)
+        prod = jnp.dot(u_ref[:, k * k_chunk:(k + 1) * k_chunk], gu_buf[(num_gu + j) % gu_slots], preferred_element_type=jnp.float32)
+        if k == 0:
+            acc_buf[rws] = prod
+        else:
+            acc_buf[rws] += prod
+        if j == num_shared_gu - 1:
+            act = (jax.nn.silu(acc_buf[:rows]) * acc_buf[rows:2 * rows]).astype(jnp.bfloat16)
+            for h in range(2):
+                shared_mid[h] = act[:, h * ff_dim:(h + 1) * ff_dim]
+
+    def shared_dn(q):
+        shared_dn_copy(q).wait()
+        cols = slice((q // 2) * col_chunk, (q // 2 + 1) * col_chunk)
+        prod = jnp.dot(shared_mid[q % 2], dn_buf[(num_dn + q) % dn_slots], preferred_element_type=jnp.float32)
+        if q % 2 == 0:
+            s_acc[:, cols] = prod
+        else:
+            s_acc[:, cols] += prod
+
+    fillers = [functools.partial(shared_gu, j) for j in range(num_shared_gu)] + [functools.partial(shared_dn, q) for q in range(num_shared_dn)]
 
     for turn in range(num_cols + half_steps + 1):
         if turn < num_cols:
@@ -338,6 +321,15 @@
             c = turn - 1 - step
             if 0 <= c < num_cols:
                 ring_step(c, step)
+                if turn >= num_cols:
+                    for filler in fillers[:2]:
+                        filler()
+                    fillers = fillers[2:]
+    for filler in fillers:
+        filler()
+    for c in range(num_cols):
+        cols = slice(c * col_chunk, (c + 1) * col_chunk)
+        out_ref[:, cols] = (a_ref[:, cols].astype(jnp.float32) + s_acc[:, cols] + part[c, 0, 0]).astype(jnp.bfloat16)
 
     for direction in range(2):
         for p in range(num_pieces):
@@ -355,17 +347,15 @@
 def moe_call(axis, num_devs, moe_in, gate_rows, resid_out, shared_gate, shared_up, shared_down, expert_gate, expert_up, expert_down, slots):
     rows, width = moe_in.shape
     local_experts, _, ff_dim = expert_gate.shape
-    shared_dim = shared_down.shape[0]
+    assert shared_down.shape[0] == 2 * ff_dim
     ring_len = num_devs // 2
     half_steps = ring_len // 2
-    shared_chunk = 256
-    shared_slots = 3
     k_chunk = min(512, width // 2)
     num_k = width // k_chunk
-    gu_slots = min(6, shared_dim // shared_chunk, local_experts * num_k)
+    gu_slots = min(10, local_experts * num_k)
     num_cols = 4
     col_chunk = width // num_cols
-    dn_slots = 8
+    dn_slots = 10
     num_pieces = 2 * half_steps - 1
     lanes = gate_rows.shape[1]
     f32, bf16 = jnp.float32, jnp.bfloat16
@@ -386,16 +376,15 @@
             pltpu.VMEM((num_devs * rows, lanes), f32),
             pltpu.VMEM((slots, 2 * ff_dim), f32),
             pltpu.VMEM((local_experts, slots, ff_dim), bf16),
+            pltpu.VMEM((2, rows, ff_dim), bf16),
             pltpu.VMEM((local_experts, slots, col_chunk), bf16),
             pltpu.VMEM((rows, width), f32),
             pltpu.VMEM((num_cols, 2, ring_len, rows, col_chunk), f32),
             pltpu.VMEM((num_cols, ring_len, rows, col_chunk), f32),
             pltpu.VMEM((2, num_cols, half_steps, rows, col_chunk), f32),
-            pltpu.VMEM((shared_slots, width, 2 * shared_chunk), bf16),
-            pltpu.VMEM((shared_slots, shared_chunk, width), bf16),
             pltpu.VMEM((gu_slots, k_chunk, 2 * ff_dim), bf16),
             pltpu.VMEM((dn_slots, ff_dim, col_chunk), bf16),
-            dma((shared_slots, 2)), dma((shared_slots,)), dma((gu_slots, 2)), dma((dn_slots,)),
+            dma((gu_slots, 2)), dma((dn_slots,)),
             dma((2, num_pieces)), dma((2, num_pieces)), dma((2, num_pieces)), dma((2, num_pieces)),
             dma((2, num_pieces + 1)), dma((2, num_pieces + 1)), dma((2, num_pieces + 1)), dma((2, num_pieces + 1)),
             dma((num_cols,)), dma((num_cols,)), dma((2, num_cols, half_steps)), dma((2, num_cols, half_steps)),

time: 98.7 us -> 96.7 us (0.980)
  Pallas kernels: 70.9 us -> 68.9 us
    pallas_call x1, Pallas kernels: 70.9 us -> 68.9 us  [moe_call(): pl.pallas_call(functools.partial(moe_kernel, axis, (num_devs, half_steps)...]
where the time goes in v2:
time: 96.7 us; the launch traced here: 96.4 us
  Pallas kernels  68.9 us (71%)
  matrix products  15.6 us (16%)
  local copies, waits for them, and re-layouts  5.71 us (6%)
  other arithmetic  5.28 us (5%)
    pallas_call x1, Pallas kernels, moe_call(): pl.pallas_call(functools.partial(moe_kernel, axis, (num_devs, half_steps)...  68.9 us
    dot_general x1, matrix products, attention_block(): jnp.dot(normed_x, w_q, preferred_element_type=jnp.float32)  7.11 us
    unnamed x35, local copies, waits for them, and re-layouts  4.77 us
    dot_general x1, matrix products, attention_block(): latent_kv = jnp.dot(normed_x, w_dkv, preferred_element_type=jnp.float32)  2.54 us

profile of v2, /device:TPU:22, one launch (start us, length us, event | category | flops | bytes accessed | tf_op | source)
XLA Modules:
  0.0 96.4 jit_solution(1310342972779625218)
XLA Ops:
  0.6 0.7 convert_element_type.61
  1.3 1.0 %fusion.14 = f32[32]{0:T(128)S(1)} fusion(bf16[32,2048]{1,0:T(8,128)(2,1)} %param.20), kind=kLoop, calls=%fused_computation.24 | loop fusion | flops 196576 | bytes 131200 | tf_op jit(solution)/shard_map/reduce_sum | solution.py:17
  2.4 2.5 %fusion.25 = f32[32,576]{1,0:T(8,128)S(1)} fusion(bf16[2048,576]{0,1:T(8,128)(2,1)} %param.29, bf16[32,2048]{1,0:T(8,128)(2,1)} %param.20, f32[2048]{0:T(1024)S(1)} %convert_element_type.61, f32[32]{0:T(128)S(1)} %add_rsqrt_fusion.2), kind=kOutput, calls=%fused_computation.44 | convolution fusion | flops 75759616 | bytes 2572416 | tf_op jit(solution)/shard_map/dot_general | solution.py:42
  4.9 0.7 convert_element_type.67
  5.6 0.1 subtract_convert_fusion.1
  5.8 7.1 %convolution_convert_fusion = bf16[32,3072]{1,0:T(8,128)(2,1)S(1)} fusion(bf16[2048,3072]{1,0:T(8,128)(2,1)} %param.28, bf16[32,2048]{1,0:T(8,128)(2,1)} %param.20, f32[2048]{0:T(1024)S(1)} %convert_element_type.61, f32[32]{0:T(128)S(1)} %add_rsqrt_fusion.2), kind=kOutput, calls=%fused_computation | convolution fusion | flops 403013632 | bytes 12918912 | tf_op jit(solution)/shard_map/dot_general | solution.py:41
  12.9 0.3 reshape.115
  13.2 0.2 subtract_convert_fusion
  13.6 0.2 fusion.28
  13.9 0.4 fusion.2
  14.3 1.1 %copy-done = bf16[32,128,512]{2,1,0:T(8,128)(2,1)S(1)} copy-done((bf16[32,128,512]{2,1,0:T(8,128)(2,1)S(1)}, bf16[32,128,512]{2,1,0:T(8,128)(2,1)}, u32[]{:S(2)}) %copy-start) | copy-done | bytes 4194328
  15.4 1.2 %fusion.9 = f32[32,16,128]{2,1,0:T(8,128)S(1)} fusion(bf16[32,128,512]{2,1,0:T(8,128)(2,1)S(1)} %copy-done, bf16[32,16,512]{2,0,1:T(8,128)(2,1)S(1)} %fusion.2), kind=kOutput, calls=%fused_computation.15 | convolution fusion | flops 67108864 | bytes 4980736 | tf_op jit(solution)/shard_map/bhc,blc->bhl/dot_general | solution.py:48
  16.6 0.1 iota_compare_fusion.1
  16.7 0.4 fusion.37
  17.1 0.1 multiply_reduce_fusion
  17.3 0.4 fusion.7
  17.7 0.2 copy-done.10
  17.9 0.2 fusion.17
  18.2 0.7 fusion.1
  19.0 0.6 fusion.5
  19.6 0.6 slice-done.1
  20.2 1.7 %fusion.11 = (f32[32]{0:T(128)S(1)}, bf16[32,2048]{1,0:T(8,128)(2,1)S(1)}) fusion(bf16[2048,2048]{1,0:T(8,128)(2,1)S(1)} %bitcast.28, bf16[16,4,8,128]{3,2,1,0:T(8,128)(2,1)S(1)} %fusion.5, bf16[32,2048]{1,0:T(8,128)(2,1)S(1)} %copy-done.1), kind=kOutput, calls=%fused_computation.21 | convolution fusion | flops 268828640 | bytes 8781952 | tf_op jit(solution)/shard_map/dot_general | solution.py:60
  21.9 0.6 copy-done.4
  22.5 0.1 fusion.13.u_ref
  22.6 0.6 copy-done.5
  23.2 0.3 fusion.38
  23.6 0.2 fusion.30
  23.8 0.1 fusion.23
  23.9 0.6 pad.4.g_ref
  24.6 68.9 %moe_ring.1 = bf16[32,2048]{1,0:T(8,128)(2,1)} custom-call(bf16[32,2048]{1,0:T(8,128)(2,1)} %copy-done.5, f32[32,128]{1,0:T(8,128)} %pad.4.g_ref, bf16[32,2048]{1,0:T(8,128)(2,1)} %copy-done.4, bf16[2048,2816]{1,0:T(8,128)(2,1)} %sg_hbm.1, bf16[2048,2816]{1,0:T(8,128)(2,1)} %su_hbm.1, bf16[2816,2048]{1,0:T(8,128)(2,1)} %sd_hbm.1, ...), custom_call_target="tpu_custom_call" | custom-call | tf_op jit(solution)/shard_map/moe_ring/pallas_call | solution.py:365
  93.5 1.4 %pad_maximum_fusion.3 = bf16[32,64]{1,0:T(8,128)(2,1)} fusion(bf16[32,32]{1,0:T(8,128)(2,1)} %copy-done.9, bf16[32,32]{1,0:T(8,128)(2,1)} %copy-done.8), kind=kLoop, calls=%fused_computation.59 | loop fusion | flops 8192 | bytes 8192 | tf_op jit(solution)/shard_map/concatenate | solution.py:31
  94.9 1.6 %copy.61 = bf16[32,2048]{1,0:T(8,128)(2,1)} copy(bf16[32,2048]{1,0:T(8,128)(2,1)} %moe_ring.1) | data formatting | bytes 262144
  (43 shorter events, 0.4 us)
Async XLA Ops:
  5.7 7.7 %copy-start.8 = (bf16[32,32]{1,0:T(8,128)(2,1)}, bf16[32,32]{1,0:T(8,128)(2,1)S(1)}, u32[]{:S(2)}) copy-start(bf16[32,32]{1,0:T(8,128)(2,1)S(1)} %get-tuple-element.7) | copy-start | bytes 6148
  5.8 7.7 %copy-start.9 = (bf16[32,32]{1,0:T(8,128)(2,1)}, bf16[32,32]{1,0:T(8,128)(2,1)S(1)}, u32[]{:S(2)}) copy-start(bf16[32,32]{1,0:T(8,128)(2,1)S(1)} %get-tuple-element.8) | copy-start | bytes 6148
  5.8 8.1 %copy-start.2 = (bf16[16,128,512]{2,1,0:T(8,128)(2,1)S(1)}, bf16[16,128,512]{2,1,0:T(8,128)(2,1)}, u32[]{:S(2)}) copy-start(bf16[16,128,512]{2,1,0:T(8,128)(2,1)} %param.30) | copy-start | bytes 6291460
  13.2 2.2 %copy-start = (bf16[32,128,512]{2,1,0:T(8,128)(2,1)S(1)}, bf16[32,128,512]{2,1,0:T(8,128)(2,1)}, u32[]{:S(2)}) copy-start(bf16[32,128,512]{2,1,0:T(8,128)(2,1)} %param.21) | copy-start | bytes 12582916
  13.4 3.2 %copy-start.14 = (s32[32]{0:T(128)S(1)}, s32[32]{0:T(128)}, u32[]{:S(2)}) copy-start(s32[32]{0:T(128)} %param.23) | copy-start | bytes 388
  13.4 3.2 %copy-start.6 = (bf16[32,128,64]{1,2,0:T(8,128)(2,1)S(1)}, bf16[32,128,64]{1,2,0:T(8,128)(2,1)}, u32[]{:S(2)}) copy-start(bf16[32,128,64]{1,2,0:T(8,128)(2,1)} %param.22) | copy-start | bytes 1572868
  13.9 3.4 %copy-start.13 = (bf16[512]{0:T(512)(128)(2,1)S(1)}, bf16[512]{0:T(512)(128)(2,1)}, u32[]{:S(2)}) copy-start(bf16[512]{0:T(512)(128)(2,1)} %param.26) | copy-start | bytes 3076
  15.4 4.2 %slice-start = ((s8[8388608]{0:T(1024)(128)(4,1)}), s8[4194304]{0:T(1024)(128)(4,1)S(1)}, s32[]{:S(2)}) async-start(s8[8388608]{0:T(1024)(128)(4,1)} %bitcast.27), calls=%async_computation | async-start | bytes 8388608
  16.6 2.4 %copy-start.3 = (bf16[16,512,128]{2,1,0:T(8,128)(2,1)S(1)}, bf16[16,512,128]{2,1,0:T(8,128)(2,1)}, u32[]{:S(2)}) copy-start(bf16[16,512,128]{2,1,0:T(8,128)(2,1)} %param.31) | copy-start | bytes 6291460
  17.3 0.6 copy-start.10
  17.7 1.9 %copy-start.1 = (bf16[32,2048]{1,0:T(8,128)(2,1)S(1)}, bf16[32,2048]{1,0:T(8,128)(2,1)}, u32[]{:S(2)}) copy-start(bf16[32,2048]{1,0:T(8,128)(2,1)} %param.20) | copy-start | bytes 393220
  17.9 2.2 %slice-start.1 = ((s8[8388608]{0:T(1024)(128)(4,1)}), s8[4194304]{0:T(1024)(128)(4,1)S(1)}, s32[]{:S(2)}) async-start(s8[8388608]{0:T(1024)(128)(4,1)} %bitcast.27), calls=%async_computation.1 | async-start | bytes 8388608
  20.2 1.7 %copy-start.11 = (bf16[2048]{0:T(1024)(128)(2,1)S(1)}, bf16[2048]{0:T(1024)(128)(2,1)}, u32[]{:S(2)}) copy-start(bf16[2048]{0:T(1024)(128)(2,1)} %param.27) | copy-start | bytes 12292
  20.2 3.1 %copy-start.7 = (bf16[2048,64]{0,1:T(8,128)(2,1)S(1)}, bf16[2048,64]{0,1:T(8,128)(2,1)}, u32[]{:S(2)}) copy-start(bf16[2048,64]{0,1:T(8,128)(2,1)} %param.33) | copy-start | bytes 786436
  20.2 3.6 %copy-start.12 = (s32[32,6]{0,1:T(8,128)S(1)}, s32[32,6]{0,1:T(8,128)}, u32[]{:S(2)}) copy-start(s32[32,6]{0,1:T(8,128)} %param.24) | copy-start | bytes 2308
  21.8 0.7 copy-start.4
  22.6 0.7 copy-start.5

commit v3 on v2

--- a/solution.py
+++ b/solution.py
@@ -1,4 +1,5 @@
 import functools
+import math
 
 import jax
 import jax.numpy as jnp
@@ -12,53 +13,188 @@
 MESH = pl.DeviceIdType.MESH
 
 
-def rms_norm(values, gain_vec):
-    vals_f32 = values.astype(jnp.float32)
-    inv_rms = lax.rsqrt(jnp.mean(vals_f32 * vals_f32, axis=-1, keepdims=True) + NORM_EPS)
-    return (vals_f32 * inv_rms * gain_vec.astype(jnp.float32)).astype(jnp.bfloat16)
-
-
-def rope_tables(positions, rope_dim):
-    inv_freq = ROPE_THETA ** (-2.0 * jnp.arange(rope_dim // 2, dtype=jnp.float32) / rope_dim)
-    angles = positions.astype(jnp.float32)[:, None] * inv_freq[None, :]
-    return jnp.cos(angles), jnp.sin(angles)
-
-
-def apply_rope(values, rope_cos, rope_sin):
-    half_dim = values.shape[-1] // 2
-    first_half = values[..., :half_dim]
-    second_half = values[..., half_dim:]
-    return jnp.concatenate([first_half * rope_cos - second_half * rope_sin, second_half * rope_cos + first_half * rope_sin], axis=-1)
-
-
-def attention_block(hidden, ckv_cache, kr_cache, seq_lens, attn_gain, kv_gain, w_q, w_dkv, w_uk, w_uv, w_o):
-    batch_rows = hidden.shape[0]
-    num_heads, nope_dim, value_a8 = w_uk.shape
-    rope_dim = kr_cache.shape[-1]
+def attn_kernel(dims, lens_smem, lens_ref, ids_ref, hid_ref, ag_ref, kg_ref, mg_ref, wq_hbm, wdkv_hbm, wuk_hbm, wuv_hbm, wo_hbm, wr_ref, ckv_hbm, kr_hbm,
+                a_ref, u_ref, g_ref, ckvn_ref, krn_ref,
+                wq, wdkv, wuk, wuv, wo, ckv, kr, q_lat, q_rot, o_lat, head_out, gate_t,
+                wq_sem, wdkv_sem, wuk_sem, wuv_sem, wo_sem, ckv_sem, kr_sem):
+    heads, nope_dim, rope_dim, latent, seq_block = dims
+    bf16, f32 = jnp.bfloat16, jnp.float32
+    rows, width = hid_ref.shape
+    cache_len = ckv_hbm.shape[1]
+    head_dim = nope_dim + rope_dim
+    v_dim = wuv_hbm.shape[2]
+    q_chunks = wq_sem.shape[0]
+    q_cols = wq_hbm.shape[1] // q_chunks
+    uk_chunks = wuk_sem.shape[0]
+    uk_heads = heads // uk_chunks
+    o_chunks = wo_sem.shape[0]
+    o_rows = wo_hbm.shape[0] // o_chunks
+    score_scale = head_dim ** -0.5
+    tiles = latent // 128
+
+    wq_cp = [pltpu.make_async_copy(wq_hbm.at[:, pl.ds(i * q_cols, q_cols)], wq.at[i], wq_sem.at[i]) for i in range(q_chunks)]
+    wdkv_cp = pltpu.make_async_copy(wdkv_hbm, wdkv, wdkv_sem)
+    wuk_cp = [pltpu.make_async_copy(wuk_hbm.at[pl.ds(i * uk_heads, uk_heads)], wuk.at[pl.ds(i * uk_heads, uk_heads)], wuk_sem.at[i]) for i in range(uk_chunks)]
+    wuv_cp = pltpu.make_async_copy(wuv_hbm, wuv, wuv_sem)
+    wo_cp = [pltpu.make_async_copy(wo_hbm.at[pl.ds(i * o_rows, o_rows)], wo.at[i], wo_sem.at[i]) for i in range(o_chunks)]
+    seq_blocks = rows // seq_block
+    ckv_cp = [pltpu.make_async_copy(ckv_hbm.at[pl.ds(i * seq_block, seq_block)], ckv.at[pl.ds(i * seq_block, seq_block)], ckv_sem.at[i]) for i in range(seq_blocks)]
+    kr_cp = pltpu.make_async_copy(kr_hbm, kr, kr_sem)
+    wdkv_cp.start()
+    for i in range(q_chunks):
+        wq_cp[i].start()
+        if i * uk_chunks % q_chunks == 0:
+            wuk_cp[i * uk_chunks // q_chunks].start()
+    kr_cp.start()
+    for cp in ckv_cp:
+        cp.start()
+    wuv_cp.start()
+    for cp in wo_cp:
+        cp.start()
+
+    def norm(vals, gain):
+        inv = lax.rsqrt(jnp.mean(vals * vals, axis=-1, keepdims=True) + NORM_EPS)
+        return (vals * inv * gain.astype(f32)).astype(bf16)
+
+    def dot_t(left, right):
+        return lax.dot_general(left, right, (((1,), (1,)), ((), ())), preferred_element_type=f32)
+
+    hid = hid_ref[...].astype(f32)
+    x = norm(hid, ag_ref[...])
+
+    lane = lax.broadcasted_iota(jnp.int32, (rows, 2 * rope_dim), 1)
+    pair = (lane % (rope_dim // 2)).astype(f32)
+    inv_freq = jnp.exp(pair * (-2.0 / rope_dim * math.log(ROPE_THETA)))
+    angles = lens_ref[...].astype(f32) * inv_freq
+    rope_cos, rope_sin = jnp.cos(angles), jnp.sin(angles)
+    first = (lane % rope_dim) < rope_dim // 2
+
+    def rope(vals):
+        swapped = jnp.where(first, -pltpu.roll(vals, 2 * rope_dim - rope_dim // 2, 1), pltpu.roll(vals, rope_dim // 2, 1))
+        return (vals * rope_cos + swapped * rope_sin).astype(bf16)
+
+    wdkv_cp.wait()
+    latent_kv = dot_t(x, wdkv[...])
+    ckv_new = norm(latent_kv[:, :latent], kg_ref[...])
+    ckvn_ref[...] = ckv_new
+    k_part = latent_kv[:, latent:latent + rope_dim]
+    kr_new = rope(jnp.concatenate([k_part, k_part], axis=1))
+    krn_ref[...] = kr_new[:, :rope_dim]
+
+    for i in range(q_chunks):
+        wq_cp[i].wait()
+        q_part = jnp.dot(x, wq[i], preferred_element_type=f32).astype(bf16).astype(f32)
+        chunk_heads = q_cols // head_dim
+        if (i * chunk_heads) % uk_heads == 0:
+            wuk_cp[i * chunk_heads // uk_heads].wait()
+        for m in range(chunk_heads // 2):
+            head = i * chunk_heads + 2 * m
+            base = 2 * m * head_dim
+            both = jnp.where(lane < rope_dim, q_part[:, base + nope_dim:base + nope_dim + 2 * rope_dim], q_part[:, base + nope_dim + 2 * rope_dim:base + 2 * head_dim])
+            turned = rope(both).astype(f32)
+            q_rot[pl.ds(head, rows, stride=heads), :] = jnp.where(lane < rope_dim, turned, 0.0)
+            q_rot[pl.ds(head + 1, rows, stride=heads), :] = jnp.where(lane < rope_dim, pltpu.roll(turned, rope_dim, 1), 0.0)
+            for h in range(2):
+                q_nope = q_part[:, base + h * head_dim:base + h * head_dim + nope_dim].astype(bf16)
+                lat = jnp.dot(q_nope, wuk[head + h], preferred_element_type=f32).astype(bf16).astype(f32)
+                for t in range(tiles):
+                    q_lat[t, pl.ds(head + h, rows, stride=heads), :] = lat[:, t * 128:(t + 1) * 128]
+
+    kr_cp.wait()
+    key_lane = lax.broadcasted_iota(jnp.int32, (heads, cache_len), 1)
+    new_lane = lax.broadcasted_iota(jnp.int32, (heads, rows), 1)
+    for i in range(seq_blocks):
+        ckv_cp[i].wait()
+
+    def attend(i, carry):
+        base = pl.multiple_of(i * seq_block * heads, seq_block * heads)
+        ql = jnp.concatenate([q_lat[t, pl.ds(base, seq_block * heads), :] for t in range(tiles)], axis=1).astype(bf16)
+        qr = q_rot[pl.ds(base, seq_block * heads), :].astype(bf16)
+        new_all = (dot_t(ql, ckv_new) + dot_t(qr[:, :rope_dim], kr_new[:, :rope_dim])) * score_scale
+        probs_new = []
+        for s in range(seq_block):
+            b = i * seq_block + s
+            part = slice(s * heads, (s + 1) * heads)
+            keys = ckv[b]
+            score = (dot_t(ql[part], keys) + jnp.dot(qr[part, :rope_dim], kr[b], preferred_element_type=f32)) * score_scale
+            score = jnp.where(key_lane < lens_smem[b], score, -jnp.inf)
+            new = jnp.where(new_lane == b, new_all[part], -jnp.inf)
+            top = jnp.maximum(jnp.max(score, axis=-1, keepdims=True), jnp.max(new, axis=-1, keepdims=True))
+            e_cache, e_new = jnp.exp(score - top), jnp.exp(new - top)
+            denom = jnp.sum(e_cache, axis=-1, keepdims=True) + jnp.sum(e_new, axis=-1, keepdims=True)
+            p_cache, p_new = (e_cache / denom).astype(bf16), (e_new / denom).astype(bf16)
+            out = jnp.dot(p_cache, keys, preferred_element_type=f32) + jnp.dot(p_new, ckv_new, preferred_element_type=f32)
+            out = out.astype(bf16).astype(f32)
+            for t in range(tiles):
+                o_lat[t, pl.ds(pl.multiple_of(base + s * heads, heads), heads), :] = out[:, t * 128:(t + 1) * 128]
+        return carry
+
+    lax.fori_loop(0, seq_blocks, attend, 0)
+
+    wuv_cp.wait()
+    for h in range(heads):
+        lat = jnp.concatenate([o_lat[t, pl.ds(h, rows, stride=heads), :] for t in range(tiles)], axis=1).astype(bf16)
+        head_out[:, h * v_dim:(h + 1) * v_dim] = jnp.dot(lat, wuv[h], preferred_element_type=f32).astype(bf16)
+
+    total = hid
+    for i in range(o_chunks):
+        wo_cp[i].wait()
+        total = total + jnp.dot(head_out[:, i * o_rows:(i + 1) * o_rows], wo[i], preferred_element_type=f32)
+    resid = total.astype(bf16)
+    a_ref[...] = resid
+    moe_in = norm(resid.astype(f32), mg_ref[...])
+    u_ref[...] = moe_in
+
+    logits = dot_t(wr_ref[...], moe_in)
+    top = jnp.max(logits, axis=0, keepdims=True)
+    e_log = jnp.exp(logits - top)
+    probs = e_log / jnp.sum(e_log, axis=0, keepdims=True)
+    expert = lax.broadcasted_iota(jnp.int32, logits.shape, 0)
+    picked = expert == ids_ref[0:1, :]
+    for k in range(1, ids_ref.shape[0]):
+        picked = picked | (expert == ids_ref[k:k + 1, :])
+    gate_t[...] = jnp.full(gate_t.shape, -1.0, f32)
+    gate_t[:logits.shape[0], :rows] = jnp.where(picked, probs, -1.0)
+    g_ref[...] = gate_t[...].T[:rows]
+
+
+def attn_call(hidden, ckv_cache, kr_cache, seq_lens, expert_ids, attn_gain, kv_gain, moe_gain, w_q, w_dkv, w_uk, w_uv, w_o, w_router):
+    rows, width = hidden.shape
+    heads, nope_dim, latent = w_uk.shape
+    v_dim = w_uv.shape[2]
+    rope_dim = kr_cache.shape[2]
     cache_len = ckv_cache.shape[1]
-    score_scale = (nope_dim + rope_dim) ** -0.5
-    normed_x = rms_norm(hidden, attn_gain)
-    q_all = jnp.dot(normed_x, w_q, preferred_element_type=jnp.float32).astype(jnp.bfloat16).reshape(batch_rows, num_heads, nope_dim + rope_dim)
-    latent_kv = jnp.dot(normed_x, w_dkv, preferred_element_type=jnp.float32)
-    ckv_new = rms_norm(latent_kv[:, :value_a8], kv_gain)
-    rope_cos, rope_sin = rope_tables(seq_lens, rope_dim)
-    kr_new = apply_rope(latent_kv[:, value_a8:], rope_cos, rope_sin).astype(jnp.bfloat16)
-    q_rot = apply_rope(q_all[:, :, nope_dim:].astype(jnp.float32), rope_cos[:, None, :], rope_sin[:, None, :]).astype(jnp.bfloat16)
-    q_lat = jnp.einsum('bhn,hnc->bhc', q_all[:, :, :nope_dim], w_uk, preferred_element_type=jnp.float32).astype(jnp.bfloat16)
-    scores = (jnp.einsum('bhc,blc->bhl', q_lat, ckv_cache, preferred_element_type=jnp.float32) + jnp.einsum('bhr,blr->bhl', q_rot, kr_cache, preferred_element_type=jnp.float32)) * score_scale
-    valid_mask = jnp.arange(cache_len)[None, None, :] < seq_lens[:, None, None]
-    scores = jnp.where(valid_mask, scores, -jnp.inf)
-    new_score = (jnp.einsum('bhc,bc->bh', q_lat, ckv_new, preferred_element_type=jnp.float32) + jnp.einsum('bhr,br->bh', q_rot, kr_new, preferred_element_type=jnp.float32)) * score_scale
-    top_score = jnp.maximum(jnp.max(scores, axis=-1), new_score)
-    exp_cache = jnp.exp(scores - top_score[:, :, None])
-    exp_new = jnp.exp(new_score - top_score)
-    denominator = jnp.sum(exp_cache, axis=-1) + exp_new
-    prob_cache = (exp_cache / denominator[:, :, None]).astype(jnp.bfloat16)
-    prob_new = (exp_new / denominator).astype(jnp.bfloat16)
-    o_lat = (jnp.einsum('bhl,blc->bhc', prob_cache, ckv_cache, preferred_element_type=jnp.float32) + jnp.einsum('bh,bc->bhc', prob_new, ckv_new, preferred_element_type=jnp.float32)).astype(jnp.bfloat16)
-    head_out = jnp.einsum('bhc,hcv->bhv', o_lat, w_uv, preferred_element_type=jnp.float32).astype(jnp.bfloat16).reshape(batch_rows, -1)
-    resid_out = (hidden.astype(jnp.float32) + jnp.dot(head_out, w_o, preferred_element_type=jnp.float32)).astype(jnp.bfloat16)
-    return resid_out, ckv_new, kr_new
+    seq_block, q_chunks, uk_chunks, o_chunks = 8, 4, 2, 4
+    bf16, f32 = jnp.bfloat16, jnp.float32
+    vmem = pl.BlockSpec(memory_space=pltpu.VMEM)
+    anym = pl.BlockSpec(memory_space=pl.ANY)
+    smem = pl.BlockSpec(memory_space=pltpu.SMEM)
+    dma = pltpu.SemaphoreType.DMA
+    shape = jax.ShapeDtypeStruct
+    return pl.pallas_call(
+        functools.partial(attn_kernel, (heads, nope_dim, rope_dim, latent, seq_block)),
+        name='attention',
+        out_shape=(shape((rows, width), bf16), shape((rows, width), bf16), shape((rows, 128), f32), shape((rows, latent), bf16), shape((rows, rope_dim), bf16)),
+        in_specs=[smem] + [vmem] * 6 + [anym] * 5 + [vmem] + [anym] * 2,
+        out_specs=(vmem,) * 5,
+        scratch_shapes=[
+            pltpu.VMEM((q_chunks, width, w_q.shape[1] // q_chunks), bf16),
+            pltpu.VMEM((w_dkv.shape[1], width), bf16),
+            pltpu.VMEM(w_uk.shape, bf16),
+            pltpu.VMEM(w_uv.shape, bf16),
+            pltpu.VMEM((o_chunks, w_o.shape[0] // o_chunks, width), bf16),
+            pltpu.VMEM((rows, cache_len, latent), bf16),
+            pltpu.VMEM((rows, rope_dim, cache_len), bf16),
+            pltpu.VMEM((latent // 128, rows * heads, 128), f32),
+            pltpu.VMEM((rows * heads, 2 * rope_dim), f32),
+            pltpu.VMEM((latent // 128, rows * heads, 128), f32),
+            pltpu.VMEM((rows, heads * v_dim), bf16),
+            pltpu.VMEM((128, 128), f32),
+            dma((q_chunks,)), dma, dma((uk_chunks,)), dma, dma((o_chunks,)), dma((rows // seq_block,)), dma,
+        ],
+        compiler_params=pltpu.CompilerParams(vmem_limit_bytes=60000000),
+    )(seq_lens, seq_lens.reshape(rows, 1), expert_ids.T, hidden, attn_gain.reshape(1, -1), kv_gain.reshape(1, -1), moe_gain.reshape(1, -1),
+      w_q, w_dkv.T, w_uk, w_uv, w_o, w_router.T, ckv_cache, kr_cache.transpose(0, 2, 1))
 
 
 def moe_kernel(axis, topo, u_ref, g_ref, a_ref, sg_hbm, su_hbm, sd_hbm, eg_hbm, eu_hbm, ed_hbm, out_ref,
@@ -393,13 +529,6 @@
     )(moe_in, gate_rows, resid_out, shared_gate, shared_up, shared_down, expert_gate, expert_up, expert_down)
 
 
-def gate_table(moe_in, expert_ids, w_router, lanes):
-    num_experts = w_router.shape[1]
-    router_prob = jax.nn.softmax(jnp.dot(moe_in, w_router, preferred_element_type=jnp.float32), axis=-1)
-    picked = jnp.any(expert_ids[:, :, None] == jnp.arange(num_experts)[None, None, :], axis=1)
-    return jnp.pad(jnp.where(picked, router_prob, -1.0), ((0, 0), (0, lanes - num_experts)), constant_values=-1.0)
-
-
 def solution(mesh):
     row_spec = P(('rep', 'dp'))
     full_spec = P()
@@ -407,13 +536,9 @@
     num_devs = mesh.shape['dp']
 
     def device_step(hidden, ckv_cache, kr_cache, seq_lens, expert_ids, attn_gain, kv_gain, moe_gain, w_q, w_dkv, w_uk, w_uv, w_o, w_router, shared_gate, shared_up, shared_down, expert_gate, expert_up, expert_down):
-        num_experts = w_router.shape[1]
-        capacity = max(2, 2 * hidden.shape[0] * expert_ids.shape[1] // num_experts)
+        capacity = max(2, 2 * hidden.shape[0] * expert_ids.shape[1] // w_router.shape[1])
         slots = -(-capacity * num_devs // 128) * 128
-        lanes = -(-num_experts // 128) * 128
-        resid_out, ckv_new, kr_new = attention_block(hidden, ckv_cache, kr_cache, seq_lens, attn_gain, kv_gain, w_q, w_dkv, w_uk, w_uv, w_o)
-        moe_in = rms_norm(resid_out, moe_gain)
-        gate_rows = gate_table(moe_in, expert_ids, w_router, lanes)
+        resid_out, moe_in, gate_rows, ckv_new, kr_new = attn_call(hidden, ckv_cache, kr_cache, seq_lens, expert_ids, attn_gain, kv_gain, moe_gain, w_q, w_dkv, w_uk, w_uv, w_o, w_router)
         layer_out = moe_call('dp', num_devs, moe_in, gate_rows, resid_out, shared_gate, shared_up, shared_down, expert_gate, expert_up, expert_down, slots)
         return layer_out, ckv_new, kr_new
 

time: 96.7 us -> 107 us (1.11)
  Pallas kernels: 68.9 us -> 99.5 us
  matrix products: 15.6 us -> 0 us
  other arithmetic: 5.28 us -> 0 us
    pallas_call x0 -> x1, Pallas kernels: none -> 30.5 us  [attn_call(): pl.pallas_call(functools.partial(attn_kernel, (heads, nope_dim, rope_dim,...]
    dot_general x11 -> x0, matrix products: 15.6 us -> none  [the longest x1 7.11 us: attention_block(): jnp.dot(normed_x, w_q, preferred_element_type=jnp.float32)]
    reshape x1 -> x4, local copies, waits for them, and re-layouts: 0.31 us -> 5.16 us  [the longest x1 1.33 us: attn_call(): seq_lens.reshape(rows, 1)]
    unnamed x35 -> x1, local copies, waits for them, and re-layouts: 4.77 us -> 1.57 us
    reduce_sum x4 -> x0, other arithmetic: 1.58 us -> none  [the longest x2 1.15 us: rms_norm(): jnp.mean(vals_f32 * vals_f32, axis=-1, keepdims=True) + NORM_EPS]
    convert_element_type x6 -> x0, other arithmetic: 1.49 us -> none  [the longest x3 0.7 us: rms_norm(): gain_vec.astype(jnp.float32)]
    concatenate x2 -> x0, other arithmetic: 1.47 us -> none  [apply_rope(): jnp.concatenate([first_half * rope_cos - second_half * rope_sin, second_h...]
where the time goes in v3:
time: 107 us
  Pallas kernels  99.5 us (93%)
  local copies, waits for them, and re-layouts  6.73 us (6%)
    pallas_call x1, Pallas kernels, moe_call(): pl.pallas_call(functools.partial(moe_kernel, axis, (num_devs, half_steps)...  69 us
    pallas_call x1, Pallas kernels, attn_call(): pl.pallas_call(functools.partial(attn_kernel, (heads, nope_dim, rope_dim,...  30.5 us

profile of v3, /device:TPU:22, one launch (start us, length us, event | category | flops | bytes accessed | tf_op | source)
XLA Modules:
  0.0 106.9 jit_solution(2136290101402824164)
XLA Ops:
  0.6 1.3 %reshape.20.kg_ref = bf16[1,512]{1,0:T(2,128)(2,1)} reshape(bf16[512]{0:T(512)(128)(2,1)} %param.26) | data formatting | bytes 2048 | tf_op jit(solution)/shard_map/reshape | solution.py:196
  1.9 1.3 %reshape.19.ag_ref = bf16[1,2048]{1,0:T(2,128)(2,1)} reshape(bf16[2048]{0:T(1024)(128)(2,1)} %param.25) | data formatting | bytes 8192 | tf_op jit(solution)/shard_map/reshape | solution.py:196
  3.2 1.3 %reshape.21.mg_ref = bf16[1,2048]{1,0:T(2,128)(2,1)} reshape(bf16[2048]{0:T(1024)(128)(2,1)} %param.27) | data formatting | bytes 8192 | tf_op jit(solution)/shard_map/reshape | solution.py:196
  4.5 1.3 %copy.23.lens_ref = s32[32,1]{1,0:T(8,128)} copy(s32[32,1]{0,1:T(1,128)} %bitcast.9) | data formatting | bytes 256 | tf_op jit(solution)/shard_map/reshape | solution.py:196
  5.8 30.5 %attention.1 = (bf16[32,2048]{1,0:T(8,128)(2,1)}, bf16[32,2048]{1,0:T(8,128)(2,1)}, f32[32,128]{1,0:T(8,128)}, bf16[32,512]{1,0:T(8,128)(2,1)}, bf16[32,64]{1,0:T(8,128)(2,1)}) custom-call(s32[32]{0:T(128)} %lens_smem.1, s32[32,1]{1,0:T(8,128)} %copy.23.lens_ref, s32[6,32]{1,0:T(8,128)} %bitcast.8, bf16[32,2048]{1,0:T(8,128)(2,1)} %hid_ref.1, ...), custom_call_target="tpu_custom_call" | custom-call | tf_op jit(solution)/shard_map/attention/pallas_call | solution.py:174
  36.3 69.0 %moe_ring.1 = bf16[32,2048]{1,0:T(8,128)(2,1)} custom-call(bf16[32,2048]{1,0:T(8,128)(2,1)} %get-tuple-element.8.u_ref, f32[32,128]{1,0:T(8,128)} %get-tuple-element.9.g_ref, bf16[32,2048]{1,0:T(8,128)(2,1)} %get-tuple-element.10.a_ref, bf16[2048,2816]{1,0:T(8,128)(2,1)} %sg_hbm.1, bf16[2048,2816]{1,0:T(8,128)(2,1)} %su_hbm.1, bf16[2816,2048]{1,0:T(8,128)(2,1)} %sd_hbm.1, ...), custom_call_target="tpu_custom_call" | custom-call | tf_op jit(solution)/shard_map/moe_ring/pallas_call | solution.py:501
  105.3 1.6 %copy.25 = bf16[32,2048]{1,0:T(8,128)(2,1)} copy(bf16[32,2048]{1,0:T(8,128)(2,1)} %moe_ring.1) | data formatting | bytes 262144

commit v4 on v3

--- a/solution.py
+++ b/solution.py
@@ -13,7 +13,7 @@
 MESH = pl.DeviceIdType.MESH
 
 
-def attn_kernel(dims, lens_smem, lens_ref, ids_ref, hid_ref, ag_ref, kg_ref, mg_ref, wq_hbm, wdkv_hbm, wuk_hbm, wuv_hbm, wo_hbm, wr_ref, ckv_hbm, kr_hbm,
+def attn_kernel(dims, lens_smem, ids_ref, hid_ref, ag_ref, kg_ref, mg_ref, wq_hbm, wdkv_hbm, wuk_hbm, wuv_hbm, wo_hbm, wr_ref, ckv_hbm, kr_hbm,
                 a_ref, u_ref, g_ref, ckvn_ref, krn_ref,
                 wq, wdkv, wuk, wuv, wo, ckv, kr, q_lat, q_rot, o_lat, head_out, gate_t,
                 wq_sem, wdkv_sem, wuk_sem, wuv_sem, wo_sem, ckv_sem, kr_sem):
@@ -40,21 +40,24 @@
     seq_blocks = rows // seq_block
     ckv_cp = [pltpu.make_async_copy(ckv_hbm.at[pl.ds(i * seq_block, seq_block)], ckv.at[pl.ds(i * seq_block, seq_block)], ckv_sem.at[i]) for i in range(seq_blocks)]
     kr_cp = pltpu.make_async_copy(kr_hbm, kr, kr_sem)
-    wdkv_cp.start()
-    for i in range(q_chunks):
-        wq_cp[i].start()
-        if i * uk_chunks % q_chunks == 0:
-            wuk_cp[i * uk_chunks // q_chunks].start()
-    kr_cp.start()
-    for cp in ckv_cp:
-        cp.start()
-    wuv_cp.start()
-    for cp in wo_cp:
-        cp.start()
+    waves = [
+        [wdkv_cp, wq_cp[0], wuk_cp[0], wq_cp[1]],
+        [wq_cp[2]],
+        [wq_cp[3], wuk_cp[1]],
+        [kr_cp, ckv_cp[0], ckv_cp[1]],
+        [wuv_cp, wo_cp[0]],
+        [wo_cp[1], wo_cp[2], wo_cp[3]],
+    ]
+
+    def start_wave(i):
+        for cp in waves[i]:
+            cp.start()
+
+    start_wave(0)
 
     def norm(vals, gain):
         inv = lax.rsqrt(jnp.mean(vals * vals, axis=-1, keepdims=True) + NORM_EPS)
-        return (vals * inv * gain.astype(f32)).astype(bf16)
+        return (vals * inv * gain.astype(f32).reshape(1, -1)).astype(bf16)
 
     def dot_t(left, right):
         return lax.dot_general(left, right, (((1,), (1,)), ((), ())), preferred_element_type=f32)
@@ -65,7 +68,11 @@
     lane = lax.broadcasted_iota(jnp.int32, (rows, 2 * rope_dim), 1)
     pair = (lane % (rope_dim // 2)).astype(f32)
     inv_freq = jnp.exp(pair * (-2.0 / rope_dim * math.log(ROPE_THETA)))
-    angles = lens_ref[...].astype(f32) * inv_freq
+    row = lax.broadcasted_iota(jnp.int32, (rows, 2 * rope_dim), 0)
+    lens = jnp.zeros((rows, 2 * rope_dim), jnp.int32)
+    for b in range(rows):
+        lens = jnp.where(row == b, lens_smem[b], lens)
+    angles = lens.astype(f32) * inv_freq
     rope_cos, rope_sin = jnp.cos(angles), jnp.sin(angles)
     first = (lane % rope_dim) < rope_dim // 2
 
@@ -74,6 +81,7 @@
         return (vals * rope_cos + swapped * rope_sin).astype(bf16)
 
     wdkv_cp.wait()
+    start_wave(1)
     latent_kv = dot_t(x, wdkv[...])
     ckv_new = norm(latent_kv[:, :latent], kg_ref[...])
     ckvn_ref[...] = ckv_new
@@ -83,6 +91,7 @@
 
     for i in range(q_chunks):
         wq_cp[i].wait()
+        start_wave(2 + i)
         q_part = jnp.dot(x, wq[i], preferred_element_type=f32).astype(bf16).astype(f32)
         chunk_heads = q_cols // head_dim
         if (i * chunk_heads) % uk_heads == 0:
@@ -101,35 +110,36 @@
                     q_lat[t, pl.ds(head + h, rows, stride=heads), :] = lat[:, t * 128:(t + 1) * 128]
 
     kr_cp.wait()
+    block_rows = seq_block * heads
     key_lane = lax.broadcasted_iota(jnp.int32, (heads, cache_len), 1)
-    new_lane = lax.broadcasted_iota(jnp.int32, (heads, rows), 1)
+    new_lane = lax.broadcasted_iota(jnp.int32, (block_rows, rows), 1)
+    new_row = lax.div(lax.broadcasted_iota(jnp.int32, (block_rows, rows), 0), heads)
+
     for i in range(seq_blocks):
         ckv_cp[i].wait()
-
-    def attend(i, carry):
-        base = pl.multiple_of(i * seq_block * heads, seq_block * heads)
-        ql = jnp.concatenate([q_lat[t, pl.ds(base, seq_block * heads), :] for t in range(tiles)], axis=1).astype(bf16)
-        qr = q_rot[pl.ds(base, seq_block * heads), :].astype(bf16)
-        new_all = (dot_t(ql, ckv_new) + dot_t(qr[:, :rope_dim], kr_new[:, :rope_dim])) * score_scale
-        probs_new = []
+        base = i * block_rows
+        ql = jnp.concatenate([q_lat[t, base:base + block_rows, :] for t in range(tiles)], axis=1).astype(bf16)
+        qr = q_rot[base:base + block_rows, :].astype(bf16)[:, :rope_dim]
+        new = (dot_t(ql, ckv_new) + dot_t(qr, kr_new[:, :rope_dim])) * score_scale
+        new = jnp.where(new_lane == new_row + i * seq_block, new, -jnp.inf)
+        scores = []
         for s in range(seq_block):
             b = i * seq_block + s
             part = slice(s * heads, (s + 1) * heads)
-            keys = ckv[b]
-            score = (dot_t(ql[part], keys) + jnp.dot(qr[part, :rope_dim], kr[b], preferred_element_type=f32)) * score_scale
-            score = jnp.where(key_lane < lens_smem[b], score, -jnp.inf)
-            new = jnp.where(new_lane == b, new_all[part], -jnp.inf)
-            top = jnp.maximum(jnp.max(score, axis=-1, keepdims=True), jnp.max(new, axis=-1, keepdims=True))
-            e_cache, e_new = jnp.exp(score - top), jnp.exp(new - top)
-            denom = jnp.sum(e_cache, axis=-1, keepdims=True) + jnp.sum(e_new, axis=-1, keepdims=True)
-            p_cache, p_new = (e_cache / denom).astype(bf16), (e_new / denom).astype(bf16)
-            out = jnp.dot(p_cache, keys, preferred_element_type=f32) + jnp.dot(p_new, ckv_new, preferred_element_type=f32)
+            score = (dot_t(ql[part], ckv[b]) + jnp.dot(qr[part], kr[b], preferred_element_type=f32)) * score_scale
+            scores.append(jnp.where(key_lane < lens_smem[b], score, -jnp.inf))
+        score = jnp.concatenate(scores, axis=0)
+        top = jnp.maximum(jnp.max(score, axis=-1, keepdims=True), jnp.max(new, axis=-1, keepdims=True))
+        e_cache, e_new = jnp.exp(score - top), jnp.exp(new - top)
+        denom = jnp.sum(e_cache, axis=-1, keepdims=True) + jnp.sum(e_new, axis=-1, keepdims=True)
+        p_cache, p_new = (e_cache / denom).astype(bf16), (e_new / denom).astype(bf16)
+        from_new = jnp.dot(p_new, ckv_new, preferred_element_type=f32)
+        for s in range(seq_block):
+            part = slice(s * heads, (s + 1) * heads)
+            out = jnp.dot(p_cache[part], ckv[i * seq_block + s], preferred_element_type=f32) + from_new[part]
             out = out.astype(bf16).astype(f32)
             for t in range(tiles):
-                o_lat[t, pl.ds(pl.multiple_of(base + s * heads, heads), heads), :] = out[:, t * 128:(t + 1) * 128]
-        return carry
-
-    lax.fori_loop(0, seq_blocks, attend, 0)
+                o_lat[t, base + s * heads:base + (s + 1) * heads, :] = out[:, t * 128:(t + 1) * 128]
 
     wuv_cp.wait()
     for h in range(heads):
@@ -145,17 +155,21 @@
     moe_in = norm(resid.astype(f32), mg_ref[...])
     u_ref[...] = moe_in
 
-    logits = dot_t(wr_ref[...], moe_in)
-    top = jnp.max(logits, axis=0, keepdims=True)
-    e_log = jnp.exp(logits - top)
-    probs = e_log / jnp.sum(e_log, axis=0, keepdims=True)
-    expert = lax.broadcasted_iota(jnp.int32, logits.shape, 0)
-    picked = expert == ids_ref[0:1, :]
-    for k in range(1, ids_ref.shape[0]):
-        picked = picked | (expert == ids_ref[k:k + 1, :])
+    half_rows = rows // 2
+    num_experts = wr_ref.shape[0]
     gate_t[...] = jnp.full(gate_t.shape, -1.0, f32)
-    gate_t[:logits.shape[0], :rows] = jnp.where(picked, probs, -1.0)
-    g_ref[...] = gate_t[...].T[:rows]
+    for half in range(2):
+        logits = dot_t(wr_ref[...], moe_in[half * half_rows:(half + 1) * half_rows])
+        top = jnp.max(logits, axis=0, keepdims=True)
+        e_log = jnp.exp(logits - top)
+        probs = e_log / jnp.sum(e_log, axis=0, keepdims=True)
+        expert = lax.broadcasted_iota(jnp.int32, logits.shape, 0)
+        ids = ids_ref[:, half * half_rows:(half + 1) * half_rows]
+        picked = expert == ids[0:1, :]
+        for k in range(1, ids.shape[0]):
+            picked = picked | (expert == ids[k:k + 1, :])
+        gate_t[half * num_experts:(half + 1) * num_experts, :half_rows] = jnp.where(picked, probs, -1.0)
+    g_ref[...] = gate_t[...].T[:half_rows]
 
 
 def attn_call(hidden, ckv_cache, kr_cache, seq_lens, expert_ids, attn_gain, kv_gain, moe_gain, w_q, w_dkv, w_uk, w_uv, w_o, w_router):
@@ -164,7 +178,7 @@
     v_dim = w_uv.shape[2]
     rope_dim = kr_cache.shape[2]
     cache_len = ckv_cache.shape[1]
-    seq_block, q_chunks, uk_chunks, o_chunks = 8, 4, 2, 4
+    seq_block, q_chunks, uk_chunks, o_chunks = rows // 2, 4, 2, 4
     bf16, f32 = jnp.bfloat16, jnp.float32
     vmem = pl.BlockSpec(memory_space=pltpu.VMEM)
     anym = pl.BlockSpec(memory_space=pl.ANY)
@@ -174,8 +188,8 @@
     return pl.pallas_call(
         functools.partial(attn_kernel, (heads, nope_dim, rope_dim, latent, seq_block)),
         name='attention',
-        out_shape=(shape((rows, width), bf16), shape((rows, width), bf16), shape((rows, 128), f32), shape((rows, latent), bf16), shape((rows, rope_dim), bf16)),
-        in_specs=[smem] + [vmem] * 6 + [anym] * 5 + [vmem] + [anym] * 2,
+        out_shape=(shape((rows, width), bf16), shape((rows, width), bf16), shape((rows // 2, 2 * w_router.shape[1]), f32), shape((rows, latent), bf16), shape((rows, rope_dim), bf16)),
+        in_specs=[smem] + [vmem] * 5 + [anym] * 5 + [vmem] + [anym] * 2,
         out_specs=(vmem,) * 5,
         scratch_shapes=[
             pltpu.VMEM((q_chunks, width, w_q.shape[1] // q_chunks), bf16),
@@ -189,11 +203,11 @@
             pltpu.VMEM((rows * heads, 2 * rope_dim), f32),
             pltpu.VMEM((latent // 128, rows * heads, 128), f32),
             pltpu.VMEM((rows, heads * v_dim), bf16),
-            pltpu.VMEM((128, 128), f32),
+            pltpu.VMEM((2 * w_router.shape[1], 128), f32),
             dma((q_chunks,)), dma, dma((uk_chunks,)), dma, dma((o_chunks,)), dma((rows // seq_block,)), dma,
         ],
         compiler_params=pltpu.CompilerParams(vmem_limit_bytes=60000000),
-    )(seq_lens, seq_lens.reshape(rows, 1), expert_ids.T, hidden, attn_gain.reshape(1, -1), kv_gain.reshape(1, -1), moe_gain.reshape(1, -1),
+    )(seq_lens, expert_ids.T, hidden, attn_gain, kv_gain, moe_gain,
       w_q, w_dkv.T, w_uk, w_uv, w_o, w_router.T, ckv_cache, kr_cache.transpose(0, 2, 1))
 
 
@@ -225,7 +239,8 @@
     slots = x_buf.shape[1] // local_experts
     num_shared_gu = 2 * num_k
     num_shared_dn = 2 * num_cols
-    num_pieces = 2 * half_steps - 1
+    half_width = width // 2
+    num_pieces = 4 * half_steps - 2
 
     def gu_copies(j):
         slot = lax.rem(j, gu_slots)
@@ -270,67 +285,72 @@
         pl.semaphore_signal(barrier, inc=1, device_id={axis: dev}, device_id_type=MESH)
     pl.semaphore_wait(barrier, 3)
 
-    def piece_rows(direction, p):
-        half = p % 2 if direction == 0 else 1 - p % 2
-        return pl.ds(half * half_rows, half_rows)
+    def piece_part(direction, p):
+        half = p % 4 // 2 if direction == 0 else 1 - p % 4 // 2
+        return pl.ds(half * half_rows, half_rows), pl.ds(p % 2 * half_width, half_width)
 
     def held_slot(direction, step):
         return (ring_len - step) % ring_len if direction == 0 else step
 
-    def gather_copies(direction, p, own):
-        step = p // 2
-        rws = piece_rows(direction, p)
-        dst = held_slot(direction, step + 1)
-        u_src = u_ref.at[rws] if own else u_all.at[0, held_slot(direction, step), rws]
-        g_src = g_ref.at[rws] if own else g_all.at[0, held_slot(direction, step), rws]
-        return (
-            pltpu.make_async_remote_copy(src_ref=u_src, dst_ref=u_all.at[0, dst, rws], send_sem=agu_send.at[direction, p], recv_sem=agu_recv.at[direction, p], device_id={axis: ring_dev[direction]}, device_id_type=MESH),
-            pltpu.make_async_remote_copy(src_ref=g_src, dst_ref=g_all.at[0, dst, rws], send_sem=agg_send.at[direction, p], recv_sem=agg_recv.at[direction, p], device_id={axis: ring_dev[direction]}, device_id_type=MESH),
-        )
-
-    def pair_copies(direction, p):
-        rws = piece_rows(direction, p)
-        slot = held_slot(direction, p // 2 + 1)
-        return (
-            pltpu.make_async_remote_copy(src_ref=u_all.at[0, slot, rws], dst_ref=u_all.at[1, slot, rws], send_sem=pru_send.at[direction, p], recv_sem=pru_recv.at[direction, p], device_id={axis: pair_dev}, device_id_type=MESH),
-            pltpu.make_async_remote_copy(src_ref=g_all.at[0, slot, rws], dst_ref=g_all.at[1, slot, rws], send_sem=prg_send.at[direction, p], recv_sem=prg_recv.at[direction, p], device_id={axis: pair_dev}, device_id_type=MESH),
-        )
+    def gather_copy(direction, p):
+        step = p // 4
+        part_of = piece_part(direction, p)
+        u_src = u_ref.at[part_of] if step == 0 else u_all.at[(0, held_slot(direction, step)) + part_of]
+        return pltpu.make_async_remote_copy(src_ref=u_src, dst_ref=u_all.at[(0, held_slot(direction, step + 1)) + part_of], send_sem=agu_send.at[direction, p], recv_sem=agu_recv.at[direction, p], device_id={axis: ring_dev[direction]}, device_id_type=MESH)
+
+    def gate_copy(direction, step):
+        g_src = g_ref if step == 0 else g_all.at[0, held_slot(direction, step)]
+        return pltpu.make_async_remote_copy(src_ref=g_src, dst_ref=g_all.at[0, held_slot(direction, step + 1)], send_sem=agg_send.at[direction, step], recv_sem=agg_recv.at[direction, step], device_id={axis: ring_dev[direction]}, device_id_type=MESH)
+
+    def pair_copy(direction, p):
+        piece = (held_slot(direction, p // 4 + 1),) + piece_part(direction, p)
+        return pltpu.make_async_remote_copy(src_ref=u_all.at[(0,) + piece], dst_ref=u_all.at[(1,) + piece], send_sem=pru_send.at[direction, p], recv_sem=pru_recv.at[direction, p], device_id={axis: pair_dev}, device_id_type=MESH)
+
+    def pair_gate_copy(direction, step):
+        slot = held_slot(direction, step + 1)
+        return pltpu.make_async_remote_copy(src_ref=g_all.at[0, slot], dst_ref=g_all.at[1, slot], send_sem=prg_send.at[direction, step], recv_sem=prg_recv.at[direction, step], device_id={axis: pair_dev}, device_id_type=MESH)
 
     pair_own = (
         pltpu.make_async_remote_copy(src_ref=u_ref, dst_ref=u_all.at[1, 0], send_sem=pru_send.at[0, num_pieces], recv_sem=pru_recv.at[0, num_pieces], device_id={axis: pair_dev}, device_id_type=MESH),
-        pltpu.make_async_remote_copy(src_ref=g_ref, dst_ref=g_all.at[1, 0], send_sem=prg_send.at[0, num_pieces], recv_sem=prg_recv.at[0, num_pieces], device_id={axis: pair_dev}, device_id_type=MESH),
+        pltpu.make_async_remote_copy(src_ref=g_ref, dst_ref=g_all.at[1, 0], send_sem=prg_send.at[0, half_steps], recv_sem=prg_recv.at[0, half_steps], device_id={axis: pair_dev}, device_id_type=MESH),
     )
-
-    for p in range(2):
+    gate_steps = (half_steps, half_steps - 1)
+
+    for p in range(4):
         for direction in range(2):
-            start_all(gather_copies(direction, p, True))
+            if p == 0:
+                gate_copy(direction, 0).start()
+            gather_copy(direction, p).start()
     start_all(pair_own)
     u_all[0, 0] = u_ref[...]
     g_all[0, 0] = g_ref[...]
 
-    def gather_event(p):
+    for p in range(num_pieces):
         for direction in range(2):
-            for cp in gather_copies(direction, p, False):
-                cp.wait_recv()
-
-        if p + 2 < num_pieces:
-            for direction in range(2):
-                start_all(gather_copies(direction, p + 2, False))
-        for direction in range(2):
-            start_all(pair_copies(direction, p))
-
-    for p in range(num_pieces):
-        gather_event(p)
+            step = p // 4
+            if p % 4 == 0 and step < gate_steps[direction]:
+                gate_copy(direction, step).wait_recv()
+                if step + 1 < gate_steps[direction]:
+                    gate_copy(direction, step + 1).start()
+                pair_gate_copy(direction, step).start()
+            gather_copy(direction, p).wait_recv()
+            if p + 4 < num_pieces:
+                gather_copy(direction, p + 4).start()
+            pair_copy(direction, p).start()
     for direction in range(2):
+        for step in range(gate_steps[direction]):
+            pair_gate_copy(direction, step).wait_recv()
         for p in range(num_pieces):
-            for cp in pair_copies(direction, p):
-                cp.wait_recv()
+            pair_copy(direction, p).wait_recv()
     for cp in pair_own:
         cp.wait_recv()
 
     total_rows = num_devs * rows
-    g_full = g_all[...].reshape(total_rows, g_all.shape[3])
-    lanes = g_full.shape[1]
+    lanes = g_all.shape[3]
+    packed = g_all[...].reshape(total_rows // 2, lanes)
+    low_half = lax.broadcasted_iota(jnp.int32, packed.shape, 1) < lanes // 2
+    halves = [jnp.where(low_half, rows_of, -1.0).reshape(num_devs, half_rows, lanes) for rows_of in (packed, pltpu.roll(packed, lanes // 2, 1))]
+    g_full = jnp.concatenate(halves, axis=1).reshape(total_rows, lanes)
     g_mine = pltpu.roll(g_full, lax.rem(lanes - me * local_experts, lanes), 1)
     g_loc[...] = jnp.maximum(g_mine, 0.0)
     hit = g_mine >= 0.0
@@ -392,11 +412,12 @@
             ahead = q + dn_slots
             if ahead < num_dn:
                 dn_copy(ahead).start()
-            else:
-                if ahead - num_dn < num_shared_gu:
-                    shared_gu_copy(ahead - num_dn).start()
-                if ahead - num_dn < num_shared_dn:
-                    shared_dn_copy(ahead - num_dn).start()
+            elif ahead - num_dn < num_shared_dn:
+                shared_dn_copy(ahead - num_dn).start()
+        for j in range(c * num_shared_gu // num_cols, (c + 1) * num_shared_gu // num_cols):
+            shared_gu_copy(j).start()
+        if c >= 1:
+            ring_step(c - 1, 0)
         total = None
         for e in range(local_experts):
             spread = jnp.dot(oht_buf[e], y_buf[e], preferred_element_type=jnp.float32) * g_loc[:, e:e + 1]
@@ -456,11 +477,12 @@
         for step in range(half_steps + 1):
             c = turn - 1 - step
             if 0 <= c < num_cols:
-                ring_step(c, step)
-                if turn >= num_cols:
-                    for filler in fillers[:2]:
-                        filler()
-                    fillers = fillers[2:]
+                if step > 0 or turn >= num_cols:
+                    ring_step(c, step)
+                run = 2 if turn >= num_cols else 0
+                for filler in fillers[:run]:
+                    filler()
+                fillers = fillers[run:]
     for filler in fillers:
         filler()
     for c in range(num_cols):
@@ -469,8 +491,11 @@
 
     for direction in range(2):
         for p in range(num_pieces):
-            for cp in gather_copies(direction, p, p < 2) + pair_copies(direction, p):
-                cp.wait_send()
+            gather_copy(direction, p).wait_send()
+            pair_copy(direction, p).wait_send()
+        for step in range(gate_steps[direction]):
+            gate_copy(direction, step).wait_send()
+            pair_gate_copy(direction, step).wait_send()
         for c in range(num_cols):
             for step in range(half_steps):
                 ring_copy(c, direction, step).wait_send()
@@ -492,7 +517,7 @@
     num_cols = 4
     col_chunk = width // num_cols
     dn_slots = 10
-    num_pieces = 2 * half_steps - 1
+    num_pieces = 4 * half_steps - 2
     lanes = gate_rows.shape[1]
     f32, bf16 = jnp.float32, jnp.bfloat16
     vmem = pl.BlockSpec(memory_space=pltpu.VMEM)
@@ -506,7 +531,7 @@
         out_specs=vmem,
         scratch_shapes=[
             pltpu.VMEM((2, ring_len, rows, width), bf16),
-            pltpu.VMEM((2, ring_len, rows, lanes), f32),
+            pltpu.VMEM((2, ring_len, rows // 2, lanes), f32),
             pltpu.VMEM((num_k, local_experts * slots, k_chunk), bf16),
             pltpu.VMEM((local_experts, num_devs * rows, slots), bf16),
             pltpu.VMEM((num_devs * rows, lanes), f32),
@@ -521,8 +546,8 @@
             pltpu.VMEM((gu_slots, k_chunk, 2 * ff_dim), bf16),
             pltpu.VMEM((dn_slots, ff_dim, col_chunk), bf16),
             dma((gu_slots, 2)), dma((dn_slots,)),
-            dma((2, num_pieces)), dma((2, num_pieces)), dma((2, num_pieces)), dma((2, num_pieces)),
-            dma((2, num_pieces + 1)), dma((2, num_pieces + 1)), dma((2, num_pieces + 1)), dma((2, num_pieces + 1)),
+            dma((2, num_pieces)), dma((2, num_pieces)), dma((2, half_steps)), dma((2, half_steps)),
+            dma((2, num_pieces + 1)), dma((2, num_pieces + 1)), dma((2, half_steps + 1)), dma((2, half_steps + 1)),
             dma((num_cols,)), dma((num_cols,)), dma((2, num_cols, half_steps)), dma((2, num_cols, half_steps)),
         ],
         compiler_params=pltpu.CompilerParams(collective_id=0, has_side_effects=True, vmem_limit_bytes=67043328),

time: 107 us -> 83.9 us (0.78)
  Pallas kernels: 99.5 us -> 81.5 us
  local copies, waits for them, and re-layouts: 6.73 us -> 1.57 us
    pallas_call x1, Pallas kernels: 30.5 us -> 15 us  [attn_call(): pl.pallas_call(functools.partial(attn_kernel, (heads, nope_dim, rope_dim,...]
    reshape x4 -> x0, local copies, waits for them, and re-layouts: 5.16 us -> none  [the longest x1 1.33 us: attn_call(): seq_lens.reshape(rows, 1)]
    pallas_call x1, Pallas kernels: 69 us -> 66.5 us  [moe_call(): pl.pallas_call(functools.partial(moe_kernel, axis, (num_devs, half_steps)...]
where the time goes in v4:
time: 83.9 us; the launch traced here: 83.7 us
  Pallas kernels  81.5 us (97%)
  local copies, waits for them, and re-layouts  1.57 us (2%)
    pallas_call x1, Pallas kernels, moe_call(): pl.pallas_call(functools.partial(moe_kernel, axis, (num_devs, half_steps)...  66.5 us
    pallas_call x1, Pallas kernels, attn_call(): pl.pallas_call(functools.partial(attn_kernel, (heads, nope_dim, rope_dim,...  15 us

profile of v4, /device:TPU:22, one launch (start us, length us, event | category | flops | bytes accessed | tf_op | source)
XLA Modules:
  0.0 83.7 jit_solution(6548614737023507322)
XLA Ops:
  0.6 15.0 %attention.1 = (bf16[32,2048]{1,0:T(8,128)(2,1)}, bf16[32,2048]{1,0:T(8,128)(2,1)}, f32[16,128]{1,0:T(8,128)}, bf16[32,512]{1,0:T(8,128)(2,1)}, bf16[32,64]{1,0:T(8,128)(2,1)}) custom-call(s32[32]{0:T(128)} %lens_smem.1, s32[6,32]{1,0:T(8,128)} %bitcast.7, bf16[32,2048]{1,0:T(8,128)(2,1)} %hid_ref.1, bf16[2048]{0:T(1024)(128)(2,1)} %ag_ref.1, ...), custom_call_target="tpu_custom_call" | custom-call | tf_op jit(solution)/shard_map/attention/pallas_call | solution.py:188
  15.6 66.5 %moe_ring.1 = bf16[32,2048]{1,0:T(8,128)(2,1)} custom-call(bf16[32,2048]{1,0:T(8,128)(2,1)} %get-tuple-element.8.u_ref, f32[16,128]{1,0:T(8,128)} %get-tuple-element.9.g_ref, bf16[32,2048]{1,0:T(8,128)(2,1)} %get-tuple-element.10.a_ref, bf16[2048,2816]{1,0:T(8,128)(2,1)} %sg_hbm.1, bf16[2048,2816]{1,0:T(8,128)(2,1)} %su_hbm.1, bf16[2816,2048]{1,0:T(8,128)(2,1)} %sd_hbm.1, ...), custom_call_target="tpu_custom_call" | custom-call | tf_op jit(solution)/shard_map/moe_ring/pallas_call | solution.py:526
  82.2 1.6 %copy.24 = bf16[32,2048]{1,0:T(8,128)(2,1)} copy(bf16[32,2048]{1,0:T(8,128)(2,1)} %moe_ring.1) | data formatting | bytes 262144

commit v5 on v4

--- a/solution.py
+++ b/solution.py
@@ -13,9 +13,9 @@
 MESH = pl.DeviceIdType.MESH
 
 
-def attn_kernel(dims, lens_smem, ids_ref, hid_ref, ag_ref, kg_ref, mg_ref, wq_hbm, wdkv_hbm, wuk_hbm, wuv_hbm, wo_hbm, wr_ref, ckv_hbm, kr_hbm,
-                a_ref, u_ref, g_ref, ckvn_ref, krn_ref,
-                wq, wdkv, wuk, wuv, wo, ckv, kr, q_lat, q_rot, o_lat, head_out, gate_t,
+def attn_kernel(dims, lens_smem, hid_ref, ag_ref, kg_ref, mg_ref, wq_hbm, wdkv_hbm, wuk_hbm, wuv_hbm, wo_hbm, ckv_hbm, kr_hbm,
+                a_ref, u_ref, ckvn_ref, krn_ref,
+                wq, wdkv, wuk, wuv, wo, ckv, kr, q_lat, q_rot, o_lat, head_out,
                 wq_sem, wdkv_sem, wuk_sem, wuv_sem, wo_sem, ckv_sem, kr_sem):
     heads, nope_dim, rope_dim, latent, seq_block = dims
     bf16, f32 = jnp.bfloat16, jnp.float32
@@ -155,24 +155,8 @@
     moe_in = norm(resid.astype(f32), mg_ref[...])
     u_ref[...] = moe_in
 
-    half_rows = rows // 2
-    num_experts = wr_ref.shape[0]
-    gate_t[...] = jnp.full(gate_t.shape, -1.0, f32)
-    for half in range(2):
-        logits = dot_t(wr_ref[...], moe_in[half * half_rows:(half + 1) * half_rows])
-        top = jnp.max(logits, axis=0, keepdims=True)
-        e_log = jnp.exp(logits - top)
-        probs = e_log / jnp.sum(e_log, axis=0, keepdims=True)
-        expert = lax.broadcasted_iota(jnp.int32, logits.shape, 0)
-        ids = ids_ref[:, half * half_rows:(half + 1) * half_rows]
-        picked = expert == ids[0:1, :]
-        for k in range(1, ids.shape[0]):
-            picked = picked | (expert == ids[k:k + 1, :])
-        gate_t[half * num_experts:(half + 1) * num_experts, :half_rows] = jnp.where(picked, probs, -1.0)
-    g_ref[...] = gate_t[...].T[:half_rows]
-
-
-def attn_call(hidden, ckv_cache, kr_cache, seq_lens, expert_ids, attn_gain, kv_gain, moe_gain, w_q, w_dkv, w_uk, w_uv, w_o, w_router):
+
+def attn_call(hidden, ckv_cache, kr_cache, seq_lens, attn_gain, kv_gain, moe_gain, w_q, w_dkv, w_uk, w_uv, w_o):
     rows, width = hidden.shape
     heads, nope_dim, latent = w_uk.shape
     v_dim = w_uv.shape[2]
@@ -188,9 +172,9 @@
     return pl.pallas_call(
         functools.partial(attn_kernel, (heads, nope_dim, rope_dim, latent, seq_block)),
         name='attention',
-        out_shape=(shape((rows, width), bf16), shape((rows, width), bf16), shape((rows // 2, 2 * w_router.shape[1]), f32), shape((rows, latent), bf16), shape((rows, rope_dim), bf16)),
-        in_specs=[smem] + [vmem] * 5 + [anym] * 5 + [vmem] + [anym] * 2,
-        out_specs=(vmem,) * 5,
+        out_shape=(shape((rows, width), bf16), shape((rows, width), bf16), shape((rows, latent), bf16), shape((rows, rope_dim), bf16)),
+        in_specs=[smem] + [vmem] * 4 + [anym] * 7,
+        out_specs=(vmem,) * 4,
         scratch_shapes=[
             pltpu.VMEM((q_chunks, width, w_q.shape[1] // q_chunks), bf16),
             pltpu.VMEM((w_dkv.shape[1], width), bf16),
@@ -203,16 +187,15 @@
             pltpu.VMEM((rows * heads, 2 * rope_dim), f32),
             pltpu.VMEM((latent // 128, rows * heads, 128), f32),
             pltpu.VMEM((rows, heads * v_dim), bf16),
-            pltpu.VMEM((2 * w_router.shape[1], 128), f32),
             dma((q_chunks,)), dma, dma((uk_chunks,)), dma, dma((o_chunks,)), dma((rows // seq_block,)), dma,
         ],
         compiler_params=pltpu.CompilerParams(vmem_limit_bytes=60000000),
-    )(seq_lens, expert_ids.T, hidden, attn_gain, kv_gain, moe_gain,
-      w_q, w_dkv.T, w_uk, w_uv, w_o, w_router.T, ckv_cache, kr_cache.transpose(0, 2, 1))
-
-
-def moe_kernel(axis, topo, u_ref, g_ref, a_ref, sg_hbm, su_hbm, sd_hbm, eg_hbm, eu_hbm, ed_hbm, out_ref,
-               u_all, g_all, x_buf, oht_buf, g_loc, acc_buf, mid_buf, shared_mid, y_buf, s_acc, part, px, ring_in,
+    )(seq_lens, hidden, attn_gain, kv_gain, moe_gain,
+      w_q, w_dkv.T, w_uk, w_uv, w_o, ckv_cache, kr_cache.transpose(0, 2, 1))
+
+
+def moe_kernel(axis, topo, u_ref, a_ref, wr_ref, ids_ref, sg_hbm, su_hbm, sd_hbm, eg_hbm, eu_hbm, ed_hbm, out_ref,
+               gate_t, g_ref, u_all, g_all, x_buf, oht_buf, g_loc, acc_buf, mid_buf, shared_mid, y_buf, s_acc, part, px, ring_in,
                gu_buf, dn_buf, gu_sem, dn_sem,
                agu_send, agu_recv, agg_send, agg_recv, pru_send, pru_recv, prg_send, prg_recv,
                px_send, px_recv, rs_send, rs_recv):
@@ -283,6 +266,22 @@
     barrier = pltpu.get_barrier_semaphore()
     for dev in (up_dev, down_dev, pair_dev):
         pl.semaphore_signal(barrier, inc=1, device_id={axis: dev}, device_id_type=MESH)
+
+    num_experts = wr_ref.shape[0]
+    gate_t[...] = jnp.full(gate_t.shape, -1.0, jnp.float32)
+    for half in range(2):
+        rws = slice(half * half_rows, (half + 1) * half_rows)
+        logits = lax.dot_general(wr_ref[...], u_ref[rws], (((1,), (1,)), ((), ())), preferred_element_type=jnp.float32)
+        top = jnp.max(logits, axis=0, keepdims=True)
+        e_log = jnp.exp(logits - top)
+        probs = e_log / jnp.sum(e_log, axis=0, keepdims=True)
+        expert = lax.broadcasted_iota(jnp.int32, logits.shape, 0)
+        ids = ids_ref[:, rws]
+        picked = expert == ids[0:1, :]
+        for k in range(1, ids.shape[0]):
+            picked = picked | (expert == ids[k:k + 1, :])
+        gate_t[half * num_experts:(half + 1) * num_experts, :half_rows] = jnp.where(picked, probs, -1.0)
+    g_ref[...] = gate_t[...].T[:half_rows]
     pl.semaphore_wait(barrier, 3)
 
     def piece_part(direction, p):
@@ -340,10 +339,7 @@
     for direction in range(2):
         for step in range(gate_steps[direction]):
             pair_gate_copy(direction, step).wait_recv()
-        for p in range(num_pieces):
-            pair_copy(direction, p).wait_recv()
-    for cp in pair_own:
-        cp.wait_recv()
+    pair_own[1].wait_recv()
 
     total_rows = num_devs * rows
     lanes = g_all.shape[3]
@@ -360,13 +356,19 @@
     rank = jnp.dot(before, jnp.where(hit, 1.0, 0.0).astype(jnp.bfloat16), preferred_element_type=jnp.float32)
     place = jnp.where(hit, rank, -1.0)
     slot_i = lax.broadcasted_iota(jnp.int32, (total_rows, slots), 1).astype(jnp.float32)
-    u_rows = u_all[...].reshape(total_rows, width)
+    picks = []
     for e in range(local_experts):
         one_hot = jnp.where(slot_i == place[:, e:e + 1], 1.0, 0.0)
         oht_buf[e] = one_hot.astype(jnp.bfloat16)
-        pick = one_hot.T.astype(jnp.bfloat16)
+        picks.append(one_hot.T.astype(jnp.bfloat16))
+    for direction in range(2):
+        for p in range(num_pieces):
+            pair_copy(direction, p).wait_recv()
+    pair_own[0].wait_recv()
+    u_rows = u_all[...].reshape(total_rows, width)
+    for e in range(local_experts):
         for k in range(num_k):
-            x_buf[k, e * slots:(e + 1) * slots] = jnp.dot(pick, u_rows[:, k * k_chunk:(k + 1) * k_chunk], preferred_element_type=jnp.float32).astype(jnp.bfloat16)
+            x_buf[k, e * slots:(e + 1) * slots] = jnp.dot(picks[e], u_rows[:, k * k_chunk:(k + 1) * k_chunk], preferred_element_type=jnp.float32).astype(jnp.bfloat16)
 
     def expert_step(e, carry):
         for k in range(num_k):
@@ -389,8 +391,12 @@
     lax.fori_loop(0, local_experts, expert_step, 0)
     half_cols = col_chunk // 2
 
-    def pair_sum_copy(c):
-        return pltpu.make_async_remote_copy(src_ref=part.at[c, 1], dst_ref=px.at[c], send_sem=px_send.at[c], recv_sem=px_recv.at[c], device_id={axis: pair_dev}, device_id_type=MESH)
+    pair_groups = ((half_steps - 1, 3), (0, half_steps - 1), (half_steps + 2, ring_len - half_steps - 2))
+
+    def pair_sum_copy(c, group):
+        first, count = pair_groups[group]
+        span = pl.ds(first, count)
+        return pltpu.make_async_remote_copy(src_ref=part.at[c, 1, span], dst_ref=px.at[c, span], send_sem=px_send.at[c, group], recv_sem=px_recv.at[c, group], device_id={axis: pair_dev}, device_id_type=MESH)
 
     def sum_slot(direction, step):
         return half_steps - step if direction == 0 else (half_steps + step) % ring_len
@@ -423,15 +429,19 @@
             spread = jnp.dot(oht_buf[e], y_buf[e], preferred_element_type=jnp.float32) * g_loc[:, e:e + 1]
             total = spread if total is None else total + spread
         part[c] = total.reshape(2, ring_len, rows, col_chunk)
-        pair_sum_copy(c).start()
+        for group in range(len(pair_groups)):
+            pair_sum_copy(c, group).start()
 
     def ring_step(c, step):
         if step == 0:
-            pair_sum_copy(c).wait_recv()
+            pair_sum_copy(c, 0).wait_recv()
             part[c, 0, half_steps] += px[c, half_steps]
             for direction in range(2):
                 ring_copy(c, direction, 0).start()
             return
+        if step == 2:
+            pair_sum_copy(c, 1).wait_recv()
+            pair_sum_copy(c, 2).wait_recv()
         for direction in range(2):
             slot = sum_slot(direction, step)
             ring_copy(c, direction, step - 1).wait_recv()
@@ -502,10 +512,11 @@
     for cp in pair_own:
         cp.wait_send()
     for c in range(num_cols):
-        pair_sum_copy(c).wait_send()
-
-
-def moe_call(axis, num_devs, moe_in, gate_rows, resid_out, shared_gate, shared_up, shared_down, expert_gate, expert_up, expert_down, slots):
+        for group in range(len(pair_groups)):
+            pair_sum_copy(c, group).wait_send()
+
+
+def moe_call(axis, num_devs, moe_in, resid_out, w_router, expert_ids, shared_gate, shared_up, shared_down, expert_gate, expert_up, expert_down, slots):
     rows, width = moe_in.shape
     local_experts, _, ff_dim = expert_gate.shape
     assert shared_down.shape[0] == 2 * ff_dim
@@ -518,7 +529,7 @@
     col_chunk = width // num_cols
     dn_slots = 10
     num_pieces = 4 * half_steps - 2
-    lanes = gate_rows.shape[1]
+    lanes = 2 * w_router.shape[1]
     f32, bf16 = jnp.float32, jnp.bfloat16
     vmem = pl.BlockSpec(memory_space=pltpu.VMEM)
     anym = pl.BlockSpec(memory_space=pl.ANY)
@@ -527,9 +538,11 @@
         functools.partial(moe_kernel, axis, (num_devs, half_steps)),
         name='moe_ring',
         out_shape=jax.ShapeDtypeStruct((rows, width), bf16),
-        in_specs=[vmem] * 3 + [anym] * 6,
+        in_specs=[vmem] * 4 + [anym] * 6,
         out_specs=vmem,
         scratch_shapes=[
+            pltpu.VMEM((lanes, 128), f32),
+            pltpu.VMEM((rows // 2, lanes), f32),
             pltpu.VMEM((2, ring_len, rows, width), bf16),
             pltpu.VMEM((2, ring_len, rows // 2, lanes), f32),
             pltpu.VMEM((num_k, local_experts * slots, k_chunk), bf16),
@@ -548,10 +561,10 @@
             dma((gu_slots, 2)), dma((dn_slots,)),
             dma((2, num_pieces)), dma((2, num_pieces)), dma((2, half_steps)), dma((2, half_steps)),
             dma((2, num_pieces + 1)), dma((2, num_pieces + 1)), dma((2, half_steps + 1)), dma((2, half_steps + 1)),
-            dma((num_cols,)), dma((num_cols,)), dma((2, num_cols, half_steps)), dma((2, num_cols, half_steps)),
+            dma((num_cols, 3)), dma((num_cols, 3)), dma((2, num_cols, half_steps)), dma((2, num_cols, half_steps)),
         ],
         compiler_params=pltpu.CompilerParams(collective_id=0, has_side_effects=True, vmem_limit_bytes=67043328),
-    )(moe_in, gate_rows, resid_out, shared_gate, shared_up, shared_down, expert_gate, expert_up, expert_down)
+    )(moe_in, resid_out, w_router.T, expert_ids.T, shared_gate, shared_up, shared_down, expert_gate, expert_up, expert_down)
 
 
 def solution(mesh):
@@ -563,8 +576,8 @@
     def device_step(hidden, ckv_cache, kr_cache, seq_lens, expert_ids, attn_gain, kv_gain, moe_gain, w_q, w_dkv, w_uk, w_uv, w_o, w_router, shared_gate, shared_up, shared_down, expert_gate, expert_up, expert_down):
         capacity = max(2, 2 * hidden.shape[0] * expert_ids.shape[1] // w_router.shape[1])
         slots = -(-capacity * num_devs // 128) * 128
-        resid_out, moe_in, gate_rows, ckv_new, kr_new = attn_call(hidden, ckv_cache, kr_cache, seq_lens, expert_ids, attn_gain, kv_gain, moe_gain, w_q, w_dkv, w_uk, w_uv, w_o, w_router)
-        layer_out = moe_call('dp', num_devs, moe_in, gate_rows, resid_out, shared_gate, shared_up, shared_down, expert_gate, expert_up, expert_down, slots)
+        resid_out, moe_in, ckv_new, kr_new = attn_call(hidden, ckv_cache, kr_cache, seq_lens, attn_gain, kv_gain, moe_gain, w_q, w_dkv, w_uk, w_uv, w_o)
+        layer_out = moe_call('dp', num_devs, moe_in, resid_out, w_router, expert_ids, shared_gate, shared_up, shared_down, expert_gate, expert_up, expert_down, slots)
         return layer_out, ckv_new, kr_new
 
     in_specs = (row_spec,) * 5 + (full_spec,) * 12 + (expert_spec,) * 3

time: 83.9 us -> 83.1 us (level)
  no operation moved by 1% of the time
where the time goes in v5:
time: 83.1 us; the launch traced here: 82.9 us
  Pallas kernels  80.7 us (97%)
  local copies, waits for them, and re-layouts  1.57 us (2%)
    pallas_call x1, Pallas kernels, moe_call(): pl.pallas_call(functools.partial(moe_kernel, axis, (num_devs, half_steps)...  66.3 us
    pallas_call x1, Pallas kernels, attn_call(): pl.pallas_call(functools.partial(attn_kernel, (heads, nope_dim, rope_dim,...  14.4 us

profile of v5, /device:TPU:22, one launch (start us, length us, event | category | flops | bytes accessed | tf_op | source)
XLA Modules:
  0.0 82.9 jit_solution(9281902698852237271)
XLA Ops:
  0.6 14.4 %attention.1 = (bf16[32,2048]{1,0:T(8,128)(2,1)}, bf16[32,2048]{1,0:T(8,128)(2,1)}, bf16[32,512]{1,0:T(8,128)(2,1)}, bf16[32,64]{1,0:T(8,128)(2,1)}) custom-call(s32[32]{0:T(128)} %lens_smem.1, bf16[32,2048]{1,0:T(8,128)(2,1)} %hid_ref.1, bf16[2048]{0:T(1024)(128)(2,1)} %ag_ref.1, bf16[512]{0:T(512)(128)(2,1)} %kg_ref.1, bf16[2048]{0:T(1024)(128)(2,1)} %mg_ref.1, ...), custom_call_target="tpu_custom_call" | custom-call | tf_op jit(solution)/shard_map/attention/pallas_call | solution.py:172
  15.0 66.3 %moe_ring.1 = bf16[32,2048]{1,0:T(8,128)(2,1)} custom-call(bf16[32,2048]{1,0:T(8,128)(2,1)} %get-tuple-element.7.u_ref, bf16[32,2048]{1,0:T(8,128)(2,1)} %get-tuple-element.8.a_ref, bf16[64,2048]{1,0:T(8,128)(2,1)} %bitcast.6, s32[6,32]{1,0:T(8,128)} %bitcast.7, bf16[2048,2816]{1,0:T(8,128)(2,1)} %sg_hbm.1, bf16[2048,2816]{1,0:T(8,128)(2,1)} %su_hbm.1, ...), custom_call_target="tpu_custom_call" | custom-call | tf_op jit(solution)/shard_map/moe_ring/pallas_call | solution.py:537
  81.3 1.6 %copy.24 = bf16[32,2048]{1,0:T(8,128)(2,1)} copy(bf16[32,2048]{1,0:T(8,128)(2,1)} %moe_ring.1) | data formatting | bytes 262144
